TPU v7x, 128 devices: a whole 4x4x4 slice. The times are simulated.
128 devices in a mesh: lat: 8 (over x_hi, y), lon: 16 (over x_lo, z, core).
Axes of the slice: x: 4 (x_hi: 2, x_lo: 2; x = x_hi * 2 + x_lo), y: 4, z: 4, core: 2. Of those that a mesh axis runs over, the one named last changes fastest.
Arguments:
- right_side: float32 [1024, 4096], P('lat', 'lon'), may hold values from -12 to 12
- diagonal: float32 [1024, 4096], P('lat', 'lon'), may hold values from 0.2 to 2
- east_coef: float32 [1024, 4096], P('lat', 'lon'), may hold values from 0.5 to 2
- north_coef: float32 [1024, 4096], P('lat', 'lon'), may hold values from 0.5 to 2
- land_sea: int32 [1024, 4096], P('lat', 'lon'), may hold values 0 or 1
- fold_partner: int32 [4096], P('lon'), may hold values from 0 to 4095, as said below
Outputs:
- solution_field: float32 [1024, 4096], P('lat', 'lon')
- residual: float32 [1024, 4096], P('lat', 'lon')
Inputs may be any that keep to these rules, and one draw needn't show every extreme that they name: fold_partner[fold_partner[i]] = i and fold_partner[i] != i for every column i, and fold_partner[i] // 256 = 15 - i // 256.
All inputs are finite; a program needn't handle non-finite values. No bound on the sum of `land_sea` on one device may be relied on, other than what follows from the above.
Results may differ from a plain program's by a relative error of at most 0.00019.
Values sent between devices are 32-bit elements; how exact they have to be, the bound alone decides.
No kernel may reach another device: no remote copies, remote signals or barrier semaphores. Data moves between devices by JAX's collectives and lax.ppermute only.
A program may use at most 64 MiB of HBM per device.

v0:
```python
import functools

import jax
import jax.numpy as jnp
from jax import lax
from jax.sharding import Mesh
from jax.sharding import PartitionSpec as P

ITERS = 4
LAT_LON = ("lat_0", "lat_1", "lon_0", "lon_1", "lon_2")
LAT = ("lat_0", "lat_1")
LON = ("lon_0", "lon_1", "lon_2")


def padded(x, sides, width):
    edges = {}
    for axis, dim in sides:
        devices, length = (lax.axis_size(axis), x.shape[dim])
        up = [(i, (i + 1) % devices) for i in range(devices)]
        last = lax.slice_in_dim(x, length - width, length, axis=dim)
        leading = lax.slice_in_dim(x, 0, width, axis=dim)
        edges[dim] = (
            lax.ppermute(last, axis, up),
            lax.ppermute(leading, axis, [(b, a) for a, b in up]),
        )
    done = []
    for _, dim in sides:
        low, high = edges[dim]
        around = [(width, width) if d in done else (0, 0) for d in range(x.ndim)]
        x = jnp.concatenate([jnp.pad(low, around), x, jnp.pad(high, around)], axis=dim)
        done.append(dim)
    return x


def over_axes(x, axes):
    return functools.reduce(lax.psum, axes, x)


def swapped(x, axis, distance):
    return lax.ppermute(x, axis, [(i, i ^ 1 << distance) for i in range(lax.axis_size(axis))])


def joint_rim(values):
    return padded(values, ((LAT, 0), (LON, 1)), 1)


def paired(residual, image):
    return (
        over_axes(jnp.sum(residual * residual), LAT_LON),
        over_axes(jnp.sum(residual * image), LAT_LON),
    )


def local(right_side, diagonal, east_coef, north_coef, land_sea, fold_partner):
    row_count, col_count = right_side.shape
    ocean = land_sea.astype(jnp.float32)
    on_top = lax.axis_index(LAT) == lax.axis_size(LAT) - 1
    row_ids = lax.broadcasted_iota(jnp.int32, (row_count, col_count), 0)
    north_inner = jnp.where(on_top & (row_ids == row_count - 1), 0.0, north_coef)
    west_coef = joint_rim(east_coef)[1:-1, :col_count]
    south_coef = joint_rim(north_inner)[:row_count, 1:-1]

    def neighbours(masked):
        framed = joint_rim(masked)
        return (
            framed[1:-1, 2:],
            framed[1:-1, :col_count],
            framed[2:, 1:-1],
            framed[:row_count, 1:-1],
        )

    lon_count = lax.axis_size(LON)
    offset = (lon_count - 1 - lax.axis_index(LON)) * col_count
    local_cols = fold_partner - offset

    def mirror_row(top_values):
        moving = top_values
        for bit_index in range(lon_count.bit_length() - 1):
            moving = swapped(moving, LON, bit_index)
        return jnp.take(moving, local_cols, axis=0)

    top_coef = north_coef[row_count - 1]
    fold_coef = jnp.where(on_top, 0.5 * (top_coef + mirror_row(top_coef)), 0.0)

    def operate(surface):
        masked = ocean * surface
        east_vals, west_vals, north_vals, south_vals = neighbours(masked)
        spread = east_coef * (masked - east_vals) + west_coef * (masked - west_vals)
        spread = spread + north_inner * (masked - north_vals) + south_coef * (masked - south_vals)
        last_row = masked[row_count - 1]
        spread = spread.at[row_count - 1].add(fold_coef * (last_row - mirror_row(last_row)))
        return diagonal * surface + ocean * spread

    solution_field = jnp.zeros_like(right_side)
    residual = right_side
    image = operate(residual)
    norm_now, product = paired(residual, image)
    alpha = norm_now / product
    direction, along = (residual, image)
    for iteration in range(ITERS):
        solution_field = solution_field + alpha * direction
        residual = residual - alpha * along
        if iteration + 1 < ITERS:
            image = operate(residual)
            norm_next, product = paired(residual, image)
            ratio = norm_next / norm_now
            alpha = norm_next / (product - ratio * norm_next / alpha)
            direction = residual + ratio * direction
            along = image + ratio * along
            norm_now = norm_next
    return (solution_field, residual)


def solution(mesh):
    torus = Mesh(mesh.devices.reshape(2, 4, 2, 4, 2), ("lat_0", "lat_1", "lon_0", "lon_1", "lon_2"))
    placed = (P(LAT, LON), P(LAT, LON), P(LAT, LON), P(LAT, LON), P(LAT, LON), P(LON))
    return jax.shard_map(
        local, mesh=torus, in_specs=placed, out_specs=(P(LAT, LON), P(LAT, LON)), check_vma=False
    )
```

profile of v0, /device:TPU:1, one launch (start us, length us, event | category | flops | bytes accessed | tf_op | source)
XLA Modules:
  0.0 249.1 jit_solution(17737360380398218637)
XLA Ops:
  9.6 3.9 %collective-permute-start.5 = (f32[1,256]{1,0:T(1,128)S(1)}, f32[1,256]{1,0:T(1,128)S(1)}, u32[]{:S(2)}, u32[]{:S(2)}) collective-permute-start(f32[1,256]{1,0:T(1,128)S(1)} %get-tuple-element.119), channel_id=1, source_target_pairs={{16,0},{32,16},{48,32},{64,48},{80,64},{96,80},{112,96},{0,112},{1... | collective-permute-start | bytes 3080 | tf_op jit(solution)/shard_map/ppermute | solution.py:24
  18.6 5.1 %collective-permute-start.1 = (f32[1,256]{1,0:T(1,128)S(1)}, f32[1,256]{1,0:T(1,128)S(1)}, u32[]{:S(2)}, u32[]{:S(2)}) collective-permute-start(f32[1,256]{1,0:T(1,128)S(1)} %get-tuple-element.122), channel_id=1, source_target_pairs={{16,0},{32,16},{48,32},{64,48},{80,64},{96,80},{112,96},{0,112},{1... | collective-permute-start | bytes 3080 | tf_op jit(solution)/shard_map/ppermute | solution.py:24
  37.0 5.9 %all-reduce.28 = (f32[]{:T(128)}, f32[]{:T(128)}) all-reduce(f32[]{:T(128)} %get-tuple-element.58, f32[]{:T(128)} %get-tuple-element.57), channel_id=1, replica_groups=mesh['lat_0'=2,'lat_1'=4,'lon_0'=2,'lon_1'=4,'lon_2'=2] {'lat_0'}, use_global_device_ids=true, to_apply=%region_1.2 | all-reduce | flops 2 | bytes 16 | tf_op jit(solution)/shard_map/psum | solution.py:36
  42.9 7.3 %all-reduce.16 = (f32[]{:T(128)}, f32[]{:T(128)}) all-reduce(f32[]{:T(128)} %get-tuple-element.97, f32[]{:T(128)} %get-tuple-element.98), channel_id=1, replica_groups=mesh['lat_0'=2,'lat_1'=4,'lon_0'=2,'lon_1'=4,'lon_2'=2] {'lat_1'}, use_global_device_ids=true, to_apply=%region_2.3 | all-reduce | flops 2 | bytes 16 | tf_op jit(solution)/shard_map/psum | solution.py:36
  50.2 4.7 %all-reduce.24 = (f32[]{:T(128)}, f32[]{:T(128)}) all-reduce(f32[]{:T(128)} %get-tuple-element.73, f32[]{:T(128)} %get-tuple-element.74), channel_id=1, replica_groups=mesh['lat_0'=2,'lat_1'=4,'lon_0'=2,'lon_1'=4,'lon_2'=2] {'lon_0'}, use_global_device_ids=true, to_apply=%region_3.4 | all-reduce | flops 2 | bytes 16 | tf_op jit(solution)/shard_map/psum | solution.py:36
  54.9 8.8 %all-reduce.12 = (f32[]{:T(128)}, f32[]{:T(128)}) all-reduce(f32[]{:T(128)} %get-tuple-element.89, f32[]{:T(128)} %get-tuple-element.90), channel_id=1, replica_groups=mesh['lat_0'=2,'lat_1'=4,'lon_0'=2,'lon_1'=4,'lon_2'=2] {'lon_1'}, use_global_device_ids=true, to_apply=%region_4.5 | all-reduce | flops 2 | bytes 16 | tf_op jit(solution)/shard_map/psum | solution.py:36
  63.7 11.6 %all-reduce.20 = (f32[]{:T(128)}, f32[]{:T(128)}) all-reduce(f32[]{:T(128)} %get-tuple-element.65, f32[]{:T(128)} %get-tuple-element.66), channel_id=1, replica_groups=mesh['lat_0'=2,'lat_1'=4,'lon_0'=2,'lon_1'=4,'lon_2'=2] {'lon_2'}, use_global_device_ids=true, to_apply=%region_5.6 | all-reduce | flops 2 | bytes 16 | tf_op jit(solution)/shard_map/psum | solution.py:36
  80.9 3.8 %collective-permute-start.17 = (f32[1,256]{1,0:T(1,128)S(1)}, f32[1,256]{1,0:T(1,128)S(1)}, u32[]{:S(2)}, u32[]{:S(2)}) collective-permute-start(f32[1,256]{1,0:T(1,128)S(1)} %get-tuple-element.116), channel_id=1, source_target_pairs={{16,0},{32,16},{48,32},{64,48},{80,64},{96,80},{112,96},{0,112},{1... | collective-permute-start | bytes 3080 | tf_op jit(solution)/shard_map/ppermute | solution.py:24
  93.8 6.0 %all-reduce.27 = (f32[]{:T(128)}, f32[]{:T(128)}) all-reduce(f32[]{:T(128)} %get-tuple-element.54, f32[]{:T(128)} %get-tuple-element.53), channel_id=1, replica_groups=mesh['lat_0'=2,'lat_1'=4,'lon_0'=2,'lon_1'=4,'lon_2'=2] {'lat_0'}, use_global_device_ids=true, to_apply=%region_13.15 | all-reduce | flops 2 | bytes 16 | tf_op jit(solution)/shard_map/psum | solution.py:36
  99.8 6.7 %all-reduce.15 = (f32[]{:T(128)}, f32[]{:T(128)}) all-reduce(f32[]{:T(128)} %get-tuple-element.95, f32[]{:T(128)} %get-tuple-element.96), channel_id=1, replica_groups=mesh['lat_0'=2,'lat_1'=4,'lon_0'=2,'lon_1'=4,'lon_2'=2] {'lat_1'}, use_global_device_ids=true, to_apply=%region_14.16 | all-reduce | flops 2 | bytes 16 | tf_op jit(solution)/shard_map/psum | solution.py:36
  106.5 4.5 %all-reduce.23 = (f32[]{:T(128)}, f32[]{:T(128)}) all-reduce(f32[]{:T(128)} %get-tuple-element.71, f32[]{:T(128)} %get-tuple-element.72), channel_id=1, replica_groups=mesh['lat_0'=2,'lat_1'=4,'lon_0'=2,'lon_1'=4,'lon_2'=2] {'lon_0'}, use_global_device_ids=true, to_apply=%region_15.17 | all-reduce | flops 2 | bytes 16 | tf_op jit(solution)/shard_map/psum | solution.py:36
  110.9 9.5 %all-reduce.11 = (f32[]{:T(128)}, f32[]{:T(128)}) all-reduce(f32[]{:T(128)} %get-tuple-element.87, f32[]{:T(128)} %get-tuple-element.88), channel_id=1, replica_groups=mesh['lat_0'=2,'lat_1'=4,'lon_0'=2,'lon_1'=4,'lon_2'=2] {'lon_1'}, use_global_device_ids=true, to_apply=%region_16.18 | all-reduce | flops 2 | bytes 16 | tf_op jit(solution)/shard_map/psum | solution.py:36
  120.5 9.3 %all-reduce.19 = (f32[]{:T(128)}, f32[]{:T(128)}) all-reduce(f32[]{:T(128)} %get-tuple-element.63, f32[]{:T(128)} %get-tuple-element.64), channel_id=1, replica_groups=mesh['lat_0'=2,'lat_1'=4,'lon_0'=2,'lon_1'=4,'lon_2'=2] {'lon_2'}, use_global_device_ids=true, to_apply=%region_17.19 | all-reduce | flops 2 | bytes 16 | tf_op jit(solution)/shard_map/psum | solution.py:36
  139.2 3.4 %collective-permute-start.25 = (f32[1,256]{1,0:T(1,128)S(1)}, f32[1,256]{1,0:T(1,128)S(1)}, u32[]{:S(2)}, u32[]{:S(2)}) collective-permute-start(f32[1,256]{1,0:T(1,128)S(1)} %get-tuple-element.112), channel_id=1, source_target_pairs={{16,0},{32,16},{48,32},{64,48},{80,64},{96,80},{112,96},{0,112},{1... | collective-permute-start | bytes 3080 | tf_op jit(solution)/shard_map/ppermute | solution.py:24
  151.6 5.9 %all-reduce.26 = (f32[]{:T(128)}, f32[]{:T(128)}) all-reduce(f32[]{:T(128)} %get-tuple-element.52, f32[]{:T(128)} %get-tuple-element.51), channel_id=1, replica_groups=mesh['lat_0'=2,'lat_1'=4,'lon_0'=2,'lon_1'=4,'lon_2'=2] {'lat_0'}, use_global_device_ids=true, to_apply=%region_25.27 | all-reduce | flops 2 | bytes 16 | tf_op jit(solution)/shard_map/psum | solution.py:36
  157.5 6.6 %all-reduce.14 = (f32[]{:T(128)}, f32[]{:T(128)}) all-reduce(f32[]{:T(128)} %get-tuple-element.93, f32[]{:T(128)} %get-tuple-element.94), channel_id=1, replica_groups=mesh['lat_0'=2,'lat_1'=4,'lon_0'=2,'lon_1'=4,'lon_2'=2] {'lat_1'}, use_global_device_ids=true, to_apply=%region_26.28 | all-reduce | flops 2 | bytes 16 | tf_op jit(solution)/shard_map/psum | solution.py:36
  164.1 4.4 %all-reduce.22 = (f32[]{:T(128)}, f32[]{:T(128)}) all-reduce(f32[]{:T(128)} %get-tuple-element.69, f32[]{:T(128)} %get-tuple-element.70), channel_id=1, replica_groups=mesh['lat_0'=2,'lat_1'=4,'lon_0'=2,'lon_1'=4,'lon_2'=2] {'lon_0'}, use_global_device_ids=true, to_apply=%region_27.29 | all-reduce | flops 2 | bytes 16 | tf_op jit(solution)/shard_map/psum | solution.py:36
  168.5 9.5 %all-reduce.10 = (f32[]{:T(128)}, f32[]{:T(128)}) all-reduce(f32[]{:T(128)} %get-tuple-element.85, f32[]{:T(128)} %get-tuple-element.86), channel_id=1, replica_groups=mesh['lat_0'=2,'lat_1'=4,'lon_0'=2,'lon_1'=4,'lon_2'=2] {'lon_1'}, use_global_device_ids=true, to_apply=%region_28.30 | all-reduce | flops 2 | bytes 16 | tf_op jit(solution)/shard_map/psum | solution.py:36
  178.0 9.2 %all-reduce.18 = (f32[]{:T(128)}, f32[]{:T(128)}) all-reduce(f32[]{:T(128)} %get-tuple-element.61, f32[]{:T(128)} %get-tuple-element.62), channel_id=1, replica_groups=mesh['lat_0'=2,'lat_1'=4,'lon_0'=2,'lon_1'=4,'lon_2'=2] {'lon_2'}, use_global_device_ids=true, to_apply=%region_29.31 | all-reduce | flops 2 | bytes 16 | tf_op jit(solution)/shard_map/psum | solution.py:36
  208.4 6.0 %all-reduce.25 = (f32[]{:T(128)}, f32[]{:T(128)}) all-reduce(f32[]{:T(128)} %get-tuple-element.56, f32[]{:T(128)} %get-tuple-element.55), channel_id=1, replica_groups=mesh['lat_0'=2,'lat_1'=4,'lon_0'=2,'lon_1'=4,'lon_2'=2] {'lat_0'}, use_global_device_ids=true, to_apply=%region_37.39 | all-reduce | flops 2 | bytes 16 | tf_op jit(solution)/shard_map/psum | solution.py:36
  214.4 6.6 %all-reduce.13 = (f32[]{:T(128)}, f32[]{:T(128)}) all-reduce(f32[]{:T(128)} %get-tuple-element.91, f32[]{:T(128)} %get-tuple-element.92), channel_id=1, replica_groups=mesh['lat_0'=2,'lat_1'=4,'lon_0'=2,'lon_1'=4,'lon_2'=2] {'lat_1'}, use_global_device_ids=true, to_apply=%region_38.40 | all-reduce | flops 2 | bytes 16 | tf_op jit(solution)/shard_map/psum | solution.py:36
  221.0 4.5 %all-reduce.21 = (f32[]{:T(128)}, f32[]{:T(128)}) all-reduce(f32[]{:T(128)} %get-tuple-element.67, f32[]{:T(128)} %get-tuple-element.68), channel_id=1, replica_groups=mesh['lat_0'=2,'lat_1'=4,'lon_0'=2,'lon_1'=4,'lon_2'=2] {'lon_0'}, use_global_device_ids=true, to_apply=%region_39.41 | all-reduce | flops 2 | bytes 16 | tf_op jit(solution)/shard_map/psum | solution.py:36
  225.4 9.5 %all-reduce.9 = (f32[]{:T(128)}, f32[]{:T(128)}) all-reduce(f32[]{:T(128)} %get-tuple-element.83, f32[]{:T(128)} %get-tuple-element.84), channel_id=1, replica_groups=mesh['lat_0'=2,'lat_1'=4,'lon_0'=2,'lon_1'=4,'lon_2'=2] {'lon_1'}, use_global_device_ids=true, to_apply=%region_40.42 | all-reduce | flops 2 | bytes 16 | tf_op jit(solution)/shard_map/psum | solution.py:36
  234.9 9.3 %all-reduce.17 = (f32[]{:T(128)}, f32[]{:T(128)}) all-reduce(f32[]{:T(128)} %get-tuple-element.59, f32[]{:T(128)} %get-tuple-element.60), channel_id=1, replica_groups=mesh['lat_0'=2,'lat_1'=4,'lon_0'=2,'lon_1'=4,'lon_2'=2] {'lon_2'}, use_global_device_ids=true, to_apply=%region_41.43 | all-reduce | flops 2 | bytes 16 | tf_op jit(solution)/shard_map/psum | solution.py:36
  (134 shorter events, 72.3 us)
Async XLA Ops:
  1.4 17.2 %collective-permute-start.4 = (f32[1,256]{1,0:T(1,128)S(1)}, f32[1,256]{1,0:T(1,128)S(1)}, u32[]{:S(2)}, u32[]{:S(2)}) collective-permute-start(f32[1,256]{1,0:T(1,128)S(1)} %get-tuple-element.118), channel_id=1, source_target_pairs={{0,16},{16,32},{32,48},{48,64},{64,80},{80,96},{96,112},{112,0},{1... | collective-permute-start | bytes 3080 | tf_op jit(solution)/shard_map/ppermute | solution.py:23
  4.2 11.2 %collective-permute-start.8 = (f32[256]{0:T(256)S(1)}, f32[256]{0:T(256)S(1)}, u32[]{:S(2)}, u32[]{:S(2)}) collective-permute-start(f32[256]{0:T(256)S(1)} %bitcast.10), channel_id=1, source_target_pairs={{0,1},{1,0},{2,3},{3,2},{4,5},{5,4},{6,7},{7,6},{8,9},{9,8},{10,11... | collective-permute-start | bytes 3080 | tf_op jit(solution)/shard_map/ppermute | solution.py:40
  8.6 8.5 %collective-permute-start.12 = (f32[256]{0:T(256)S(1)}, f32[256]{0:T(256)S(1)}, u32[]{:S(2)}, u32[]{:S(2)}) collective-permute-start(f32[256]{0:T(256)S(1)} %bitcast.12), channel_id=1, source_target_pairs={{0,1},{1,0},{2,3},{3,2},{4,5},{5,4},{6,7},{7,6},{8,9},{9,8},{10,11... | collective-permute-start | bytes 3080 | tf_op jit(solution)/shard_map/ppermute | solution.py:40
  8.8 4.7 %collective-permute-start.2 = (f32[128,1]{1,0:T(8,128)S(1)}, f32[128,1]{1,0:T(8,128)S(1)}, u32[]{:S(2)}, u32[]{:S(2)}) collective-permute-start(f32[128,1]{1,0:T(8,128)S(1)} %get-tuple-element.120), channel_id=1, source_target_pairs={{1,0},{2,1},{3,2},{4,3},{5,4},{6,5},{7,6},{8,7},{9,8},{10,9},{11,1... | collective-permute-start | bytes 1544 | tf_op jit(solution)/shard_map/ppermute | solution.py:24
  9.6 9.0 %collective-permute-start.5 = (f32[1,256]{1,0:T(1,128)S(1)}, f32[1,256]{1,0:T(1,128)S(1)}, u32[]{:S(2)}, u32[]{:S(2)}) collective-permute-start(f32[1,256]{1,0:T(1,128)S(1)} %get-tuple-element.119), channel_id=1, source_target_pairs={{16,0},{32,16},{48,32},{64,48},{80,64},{96,80},{112,96},{0,112},{1... | collective-permute-start | bytes 3080 | tf_op jit(solution)/shard_map/ppermute | solution.py:24
  13.5 5.1 %collective-permute-start.6 = (f32[128,1]{1,0:T(8,128)S(1)}, f32[128,1]{1,0:T(8,128)S(1)}, u32[]{:S(2)}, u32[]{:S(2)}) collective-permute-start(f32[128,1]{1,0:T(8,128)S(1)} %get-tuple-element.121), channel_id=1, source_target_pairs={{0,1},{1,2},{2,3},{3,4},{4,5},{5,6},{6,7},{7,8},{8,9},{9,10},{10,1... | collective-permute-start | bytes 1544 | tf_op jit(solution)/shard_map/ppermute | solution.py:23
  15.4 8.3 %collective-permute-start.9 = (f32[256]{0:T(256)S(1)}, f32[256]{0:T(256)S(1)}, u32[]{:S(2)}, u32[]{:S(2)}) collective-permute-start(f32[256]{0:T(256)S(1)} %collective-permute-done.8), channel_id=1, source_target_pairs={{0,2},{1,3},{2,0},{3,1},{4,6},{5,7},{6,4},{7,5},{8,10},{9,11},{10,... | collective-permute-start | bytes 3080 | tf_op jit(solution)/shard_map/ppermute | solution.py:40
  17.1 9.0 %collective-permute-start.13 = (f32[256]{0:T(256)S(1)}, f32[256]{0:T(256)S(1)}, u32[]{:S(2)}, u32[]{:S(2)}) collective-permute-start(f32[256]{0:T(256)S(1)} %collective-permute-done.12), channel_id=1, source_target_pairs={{0,2},{1,3},{2,0},{3,1},{4,6},{5,7},{6,4},{7,5},{8,10},{9,11},{10,... | collective-permute-start | bytes 3080 | tf_op jit(solution)/shard_map/ppermute | solution.py:40
  18.6 13.5 %collective-permute-start = (f32[1,256]{1,0:T(1,128)S(1)}, f32[1,256]{1,0:T(1,128)S(1)}, u32[]{:S(2)}, u32[]{:S(2)}) collective-permute-start(f32[1,256]{1,0:T(1,128)S(1)} %get-tuple-element.123), channel_id=1, source_target_pairs={{0,16},{16,32},{32,48},{48,64},{64,80},{80,96},{96,112},{112,0},{1... | collective-permute-start | bytes 3080 | tf_op jit(solution)/shard_map/ppermute | solution.py:23
  18.6 13.5 %collective-permute-start.7 = (f32[1,256]{1,0:T(1,128)S(1)}, f32[1,256]{1,0:T(1,128)S(1)}, u32[]{:S(2)}, u32[]{:S(2)}) collective-permute-start(f32[1,256]{1,0:T(1,128)S(1)} %slice.266), channel_id=1, source_target_pairs={{0,16},{16,32},{32,48},{48,64},{64,80},{80,96},{96,112},{112,0},{1... | collective-permute-start | bytes 3080 | tf_op jit(solution)/shard_map/ppermute | solution.py:23
  18.6 13.5 %collective-permute-start.1 = (f32[1,256]{1,0:T(1,128)S(1)}, f32[1,256]{1,0:T(1,128)S(1)}, u32[]{:S(2)}, u32[]{:S(2)}) collective-permute-start(f32[1,256]{1,0:T(1,128)S(1)} %get-tuple-element.122), channel_id=1, source_target_pairs={{16,0},{32,16},{48,32},{64,48},{80,64},{96,80},{112,96},{0,112},{1... | collective-permute-start | bytes 3080 | tf_op jit(solution)/shard_map/ppermute | solution.py:24
  26.1 4.2 %collective-permute-start.14 = (f32[256]{0:T(256)S(1)}, f32[256]{0:T(256)S(1)}, u32[]{:S(2)}, u32[]{:S(2)}) collective-permute-start(f32[256]{0:T(256)S(1)} %collective-permute-done.13), channel_id=1, source_target_pairs={{0,4},{1,5},{2,6},{3,7},{4,0},{5,1},{6,2},{7,3},{8,12},{9,13},{10,... | collective-permute-start | bytes 3080 | tf_op jit(solution)/shard_map/ppermute | solution.py:40
  27.7 4.6 %collective-permute-start.11 = (f32[256]{0:T(256)S(1)}, f32[256]{0:T(256)S(1)}, u32[]{:S(2)}, u32[]{:S(2)}) collective-permute-start(f32[256]{0:T(256)S(1)} %collective-permute-done.10), channel_id=1, source_target_pairs={{0,8},{1,9},{2,10},{3,11},{4,12},{5,13},{6,14},{7,15},{8,0},{9,1},... | collective-permute-start | bytes 3080 | tf_op jit(solution)/shard_map/ppermute | solution.py:40
  77.9 6.8 %collective-permute-start.21 = (f32[256]{0:T(256)S(1)}, f32[256]{0:T(256)S(1)}, u32[]{:S(2)}, u32[]{:S(2)}) collective-permute-start(f32[256]{0:T(256)S(1)} %collective-permute-done.20), channel_id=1, source_target_pairs={{0,2},{1,3},{2,0},{3,1},{4,6},{5,7},{6,4},{7,5},{8,10},{9,11},{10,... | collective-permute-start | bytes 3080 | tf_op jit(solution)/shard_map/ppermute | solution.py:40
  79.6 10.4 %collective-permute-start.16 = (f32[1,256]{1,0:T(1,128)S(1)}, f32[1,256]{1,0:T(1,128)S(1)}, u32[]{:S(2)}, u32[]{:S(2)}) collective-permute-start(f32[1,256]{1,0:T(1,128)S(1)} %get-tuple-element.117), channel_id=1, source_target_pairs={{0,16},{16,32},{32,48},{48,64},{64,80},{80,96},{96,112},{112,0},{1... | collective-permute-start | bytes 3080 | tf_op jit(solution)/shard_map/ppermute | solution.py:23
  80.9 9.1 %collective-permute-start.17 = (f32[1,256]{1,0:T(1,128)S(1)}, f32[1,256]{1,0:T(1,128)S(1)}, u32[]{:S(2)}, u32[]{:S(2)}) collective-permute-start(f32[1,256]{1,0:T(1,128)S(1)} %get-tuple-element.116), channel_id=1, source_target_pairs={{16,0},{32,16},{48,32},{64,48},{80,64},{96,80},{112,96},{0,112},{1... | collective-permute-start | bytes 3080 | tf_op jit(solution)/shard_map/ppermute | solution.py:24
  86.0 4.0 %collective-permute-start.18 = (f32[128,1]{1,0:T(8,128)S(1)}, f32[128,1]{1,0:T(8,128)S(1)}, u32[]{:S(2)}, u32[]{:S(2)}) collective-permute-start(f32[128,1]{1,0:T(8,128)S(1)} %get-tuple-element.114), channel_id=1, source_target_pairs={{1,0},{2,1},{3,2},{4,3},{5,4},{6,5},{7,6},{8,7},{9,8},{10,9},{11,1... | collective-permute-start | bytes 1544 | tf_op jit(solution)/shard_map/ppermute | solution.py:24
  135.7 6.8 %collective-permute-start.29 = (f32[256]{0:T(256)S(1)}, f32[256]{0:T(256)S(1)}, u32[]{:S(2)}, u32[]{:S(2)}) collective-permute-start(f32[256]{0:T(256)S(1)} %collective-permute-done.28), channel_id=1, source_target_pairs={{0,2},{1,3},{2,0},{3,1},{4,6},{5,7},{6,4},{7,5},{8,10},{9,11},{10,... | collective-permute-start | bytes 3080 | tf_op jit(solution)/shard_map/ppermute | solution.py:40
  137.4 10.4 %collective-permute-start.24 = (f32[1,256]{1,0:T(1,128)S(1)}, f32[1,256]{1,0:T(1,128)S(1)}, u32[]{:S(2)}, u32[]{:S(2)}) collective-permute-start(f32[1,256]{1,0:T(1,128)S(1)} %get-tuple-element.113), channel_id=1, source_target_pairs={{0,16},{16,32},{32,48},{48,64},{64,80},{80,96},{96,112},{112,0},{1... | collective-permute-start | bytes 3080 | tf_op jit(solution)/shard_map/ppermute | solution.py:23
  139.2 8.7 %collective-permute-start.25 = (f32[1,256]{1,0:T(1,128)S(1)}, f32[1,256]{1,0:T(1,128)S(1)}, u32[]{:S(2)}, u32[]{:S(2)}) collective-permute-start(f32[1,256]{1,0:T(1,128)S(1)} %get-tuple-element.112), channel_id=1, source_target_pairs={{16,0},{32,16},{48,32},{64,48},{80,64},{96,80},{112,96},{0,112},{1... | collective-permute-start | bytes 3080 | tf_op jit(solution)/shard_map/ppermute | solution.py:24
  192.6 6.8 %collective-permute-start.37 = (f32[256]{0:T(256)S(1)}, f32[256]{0:T(256)S(1)}, u32[]{:S(2)}, u32[]{:S(2)}) collective-permute-start(f32[256]{0:T(256)S(1)} %collective-permute-done.36), channel_id=1, source_target_pairs={{0,2},{1,3},{2,0},{3,1},{4,6},{5,7},{6,4},{7,5},{8,10},{9,11},{10,... | collective-permute-start | bytes 3080 | tf_op jit(solution)/shard_map/ppermute | solution.py:40
  194.3 10.4 %collective-permute-start.32 = (f32[1,256]{1,0:T(1,128)S(1)}, f32[1,256]{1,0:T(1,128)S(1)}, u32[]{:S(2)}, u32[]{:S(2)}) collective-permute-start(f32[1,256]{1,0:T(1,128)S(1)} %get-tuple-element.109), channel_id=1, source_target_pairs={{0,16},{16,32},{32,48},{48,64},{64,80},{80,96},{96,112},{112,0},{1... | collective-permute-start | bytes 3080 | tf_op jit(solution)/shard_map/ppermute | solution.py:23
  196.0 8.7 %collective-permute-start.33 = (f32[1,256]{1,0:T(1,128)S(1)}, f32[1,256]{1,0:T(1,128)S(1)}, u32[]{:S(2)}, u32[]{:S(2)}) collective-permute-start(f32[1,256]{1,0:T(1,128)S(1)} %get-tuple-element.108), channel_id=1, source_target_pairs={{16,0},{32,16},{48,32},{64,48},{80,64},{96,80},{112,96},{0,112},{1... | collective-permute-start | bytes 3080 | tf_op jit(solution)/shard_map/ppermute | solution.py:24
  200.6 4.0 %collective-permute-start.34 = (f32[128,1]{1,0:T(8,128)S(1)}, f32[128,1]{1,0:T(8,128)S(1)}, u32[]{:S(2)}, u32[]{:S(2)}) collective-permute-start(f32[128,1]{1,0:T(8,128)S(1)} %get-tuple-element.106), channel_id=1, source_target_pairs={{1,0},{2,1},{3,2},{4,3},{5,4},{6,5},{7,6},{8,7},{9,8},{10,9},{11,1... | collective-permute-start | bytes 1544 | tf_op jit(solution)/shard_map/ppermute | solution.py:24
  (22 other events, 88.0 us)
where the time goes:
time: 250 us; the launch traced here: 249 us
  blocking collectives  145 us (58%)
  starting transfers between devices  58.5 us (23%)
  between operations  15.2 us (6%)
  local copies, waits for them, and re-layouts  12.8 us (5%)
  waiting for transfers between devices  11.5 us (5%)
  other arithmetic  5.75 us (2%)
    psum x20, blocking collectives, over_axes(): return functools.reduce(lax.psum, axes, x)  145 us
    ppermute x9, starting transfers between devices, padded(): lax.ppermute(leading, axis, [(b, a) for a, b in up])  24.6 us
    ppermute x20, starting transfers between devices, swapped(): lax.ppermute(x, axis, [(i, i ^ 1 << distance) for i in range(lax.axis_siz...  22.7 us
    ppermute x11, starting transfers between devices, padded(): lax.ppermute(last, axis, up)  11.2 us
    gather x5, local copies, waits for them, and re-layouts, mirror_row(): return jnp.take(moving, local_cols, axis=0)  9.71 us
    ppermute x20, waiting for transfers between devices, swapped(): lax.ppermute(x, axis, [(i, i ^ 1 << distance) for i in range(lax.axis_siz...  9.47 us
  transfers between devices with their start and end apart: 40, of which 15 were waited for; matrix products, arithmetic and copies ran while one was open for 2% of the time, Pallas kernels for 0%

commit v1 on v0

v1 whole, which is shorter than its diff:
```python
import functools

import jax
import jax.numpy as jnp
from jax import lax
from jax.experimental import pallas as pl
from jax.experimental.pallas import tpu as pltpu
from jax.sharding import Mesh
from jax.sharding import PartitionSpec as P

ITERS = 4
LAT_LON = ("lat_0", "lat_1", "lon_0", "lon_1", "lon_2")
LAT = ("lat_0", "lat_1")
LON = ("lon_0", "lon_1", "lon_2")
MID = 4.6
HALF = 4.4
F32 = jnp.float32
W = 4
LANES = 128
STRIP = 48


def _iota(shape, axis):
    return lax.broadcasted_iota(jnp.int32, shape, axis)


def _cat(parts, axis):
    return jnp.concatenate(parts, axis=axis)


def _pack_rows(*refs):
    bottoms, tops, (partner, south_out, north_out) = (refs[:5], refs[5:10], refs[10:])
    south_out[...] = jnp.zeros_like(south_out)
    north_out[...] = jnp.zeros_like(north_out)
    for f in range(5):
        south_out[W * f : W * f + W, :] = bottoms[f][0:W, :].astype(F32)
        north_out[W * f : W * f + W, :] = tops[f][8 - W : 8, :].astype(F32)
    north_out[20:21, :] = partner[...].astype(F32)


def pack_rows(fields, partner):
    rows, cols = fields[0].shape
    low = pl.BlockSpec((8, cols), lambda i: (0, 0))
    high = pl.BlockSpec((8, cols), lambda i: (rows // 8 - 1, 0))
    out = jax.ShapeDtypeStruct((24, cols), F32)
    return pl.pallas_call(
        _pack_rows,
        grid=(1,),
        in_specs=[low] * 5 + [high] * 5 + [pl.BlockSpec((1, cols), lambda i: (0, 0))],
        out_specs=(pl.BlockSpec((24, cols), lambda i: (0, 0)),) * 2,
        out_shape=(out, out),
        name="pack_rows",
    )(*fields, *fields, partner)


def _pick(source, index):
    low = index & (LANES - 1)
    outs = []
    for t in range(2):
        at = low[:, t * LANES : (t + 1) * LANES]
        first = jnp.take_along_axis(source[:, :LANES], at, axis=1)
        second = jnp.take_along_axis(source[:, LANES:], at, axis=1)
        outs.append(jnp.where(index[:, t * LANES : (t + 1) * LANES] < LANES, first, second))
    return _cat(outs, 1)


def _pack_cols(top, r, oc, dg, ea, no, from_n, from_s, from_m, own_top, to_w, to_e, strip):
    rows = r.shape[0]
    lane = _iota((1, LANES), 1)

    def packed(pieces):
        west = east = None
        for f, (left, right) in enumerate(pieces):
            a = left if f == 0 else pltpu.roll(left, W * f, 1)
            b = pltpu.roll(right, W * f + W, 1)
            if f == 0:
                west, east = (a, b)
            else:
                here = lane >= W * f
                west = jnp.where(here, a, west)
                east = jnp.where(here, b, east)
        used = lane < 5 * W
        return (jnp.where(used, west, 0.0), jnp.where(used, east, 0.0))

    zero = jnp.zeros((W, LANES), F32)
    for start in range(0, rows, 32):
        span = pl.ds(start, 32)
        west, east = packed(
            [(x[span, :LANES].astype(F32), x[span, LANES:].astype(F32)) for x in (r, oc, dg, ea, no)]
        )
        to_w[pl.ds(8 + start, 32), :] = west
        to_e[pl.ds(8 + start, 32), :] = east
    for src, base, blank in ((from_s, 4, 0), (from_n, 8 + rows, 12 + rows)):
        west, east = packed(
            [(src[W * f : W * f + W, :LANES], src[W * f : W * f + W, LANES:]) for f in range(5)]
        )
        to_w[base : base + W, :] = west
        to_e[base : base + W, :] = east
        to_w[blank : blank + W, :] = zero
        to_e[blank : blank + W, :] = zero

    @pl.when(top[0] == 1)
    def _():
        for f in range(5):
            strip[8 * f : 8 * f + W, :] = own_top[W * f : W * f + W, :]
            strip[8 * f + W : 8 * f + 8, :] = from_m[W * f : W * f + W, :]
        strip[40:48, :] = jnp.zeros((8, 2 * LANES), F32)
        own_partner, far_partner = (own_top[20:21, :], from_m[20:21, :])
        strip[40:41, :] = own_partner
        strip[41:42, :] = far_partner
        row = _iota((8, 1), 0)
        index = jnp.where(row < 4, own_partner, far_partner).astype(jnp.int32) & (2 * LANES - 1)
        masked = strip[0:8, :] * strip[8:16, :]
        first = _pick(pltpu.roll(masked, 4, 0), index)
        north = strip[32:40, :]
        coef = 0.5 * (north + _pick(pltpu.roll(north, 4, 0), index))
        strip[35:36, :] = coef[3:4, :]
        strip[39:40, :] = coef[7:8, :]
        strip[42:43, :] = first[3:4, :]
        strip[43:44, :] = first[7:8, :]

    base = rows + 16
    for half in range(2):
        part = strip[:, half * LANES : (half + 1) * LANES]
        to_w[base + STRIP * half : base + STRIP * (half + 1), :] = part
        to_e[base + STRIP * half : base + STRIP * (half + 1), :] = part


def pack_cols(top, fields, from_n, from_s, from_m, own_top):
    rows, cols = fields[0].shape
    message = jax.ShapeDtypeStruct((rows + 16 + 2 * STRIP, LANES), F32)
    vmem = pl.BlockSpec(memory_space=pltpu.VMEM)
    return pl.pallas_call(
        _pack_cols,
        in_specs=[pl.BlockSpec(memory_space=pltpu.SMEM)] + [vmem] * 9,
        out_specs=(vmem,) * 3,
        out_shape=(message, message, jax.ShapeDtypeStruct((STRIP, cols), F32)),
        name="pack_cols",
    )(top, *fields, from_n, from_s, from_m, own_top)


def _lanes_left(x):
    return pltpu.roll(x, x.shape[1] - 1, 1)


def _lanes_right(x):
    return pltpu.roll(x, 1, 1)


def _strip_levels(strip, from_e, from_w, e2, w2, fold, base):
    row = _iota((8, 1), 0)
    lane = _iota((1, LANES), 1)
    near = row < 4

    def far(ref, at, count):
        return _cat(
            [ref[base + at : base + at + count, :], ref[base + STRIP + at : base + STRIP + at + count, :]], 1
        )

    def assembled(mine, east, west, east2, west2):
        left = jnp.where(near, west, east)
        right = jnp.where(near, east, west)
        tail = jnp.where(
            lane < 64,
            jnp.where(near, east2, west2)[:, :LANES],
            jnp.where(near, west2, east2)[:, LANES:],
        )
        return _cat([left, mine, right, tail], 1)

    def field(f):
        s = 8 * f
        return assembled(
            strip[s : s + 8, :], far(from_e, s, 8), far(from_w, s, 8), e2[s : s + 8, :], w2[s : s + 8, :]
        )

    def pair(at):
        def one(a, b):
            return jnp.where(near, a, b)

        return assembled(
            one(strip[at : at + 1, :], strip[at + 1 : at + 2, :]),
            one(far(from_e, at, 1), far(from_e, at + 1, 1)),
            one(far(from_w, at, 1), far(from_w, at + 1, 1)),
            one(e2[at : at + 1, :], e2[at + 1 : at + 2, :]),
            one(w2[at : at + 1, :], w2[at + 1 : at + 2, :]),
        )

    r, oc, dg, ea, no = [field(f) for f in range(5)]
    index = pair(40).astype(jnp.int32) & (2 * LANES - 1)
    neighbour = pair(42)
    edge = (row & 3) == 3
    fc = jnp.where(edge, no, 0.0)
    no = jnp.where(edge, 0.0, no)
    scale = 2.0 / HALF
    ocs = oc * scale
    ce = ea * ocs * _lanes_left(oc)
    cw = _lanes_right(ce)
    cn = no * ocs * pltpu.roll(oc, 7, 0)
    cs = pltpu.roll(cn, 1, 0)
    cf = fc * ocs
    d = (dg - MID) * scale + ocs * (ea + _lanes_right(ea) + no + pltpu.roll(no, 1, 0) + fc)

    def main_row(x):
        x = x[3:4, :]
        return _cat([x[:, 256:512], jnp.where(lane < 64, x[:, 512:640], x[:, 128:256])], 1)

    fold[4:5, :] = main_row(cf)
    previous = None
    value = r
    for k in range(4):
        term = cf * neighbour
        fold[k : k + 1, :] = main_row(term)
        if k == 3:
            break
        new = (
            d * value
            - ce * _lanes_left(value)
            - cw * _lanes_right(value)
            - cn * pltpu.roll(value, 7, 0)
            - cs * pltpu.roll(value, 1, 0)
            - term
        )
        new = 0.5 * new if k == 0 else new - previous
        previous, value = (value, new)
        swapped = pltpu.roll(value * oc, 4, 0)
        blocks = [swapped[:, 256 * j : 256 * j + 256] for j in range(3)]
        picked = [_pick(blocks[2 - j], index[:, 256 * j : 256 * j + 256]) for j in range(3)]
        neighbour = _cat([*picked, jnp.zeros((8, LANES), F32)], 1)


def _basis(top, r, oc, dg, ea, no, from_n, from_s, from_e, from_w, strip, e2, w2, t1, t2, t3, t4, moments, ext, coef, fold):
    rows, cols = r.shape
    pad = 16
    high = rows + pad
    wide = cols + LANES
    lane = _iota((1, LANES), 1)
    total = rows + 2 * pad
    on_top = top[0] == 1
    for f, own in enumerate((r, oc, dg, ea, no)):
        ext[f, 0 : pad, :cols] = jnp.zeros((pad, cols), F32)
        ext[f, high : high + pad, :cols] = jnp.zeros((pad, cols), F32)
        ext[f, pad:high, :cols] = own[...].astype(F32)
        ext[f, pad - W : pad, :cols] = from_s[W * f : W * f + W, :]
        ext[f, high : high + W, :cols] = from_n[W * f : W * f + W, :]
        ext[f, 0:8, cols:] = jnp.zeros((8, LANES), F32)
        ext[f, total - 8 : total, cols:] = jnp.zeros((8, LANES), F32)
        east = from_e[0 : rows + 16, :]
        if f:
            east = pltpu.roll(east, LANES - W * f, 1)
        west = pltpu.roll(from_w[0 : rows + 16, :], LANES - W - W * f, 1)
        halo = jnp.where(lane < W, east, jnp.where(lane >= LANES - W, west, 0.0))
        ext[f, 8 : 8 + rows + 16, cols:] = halo
    for k in (5, 6, 7):
        ext[k, 0:8, :] = jnp.zeros((8, wide), F32)
        ext[k, total - 8 : total, :] = jnp.zeros((8, wide), F32)

    @pl.when(on_top)
    def _():
        ext[4, high - 1 : high, :] = jnp.zeros((1, wide), F32)
        _strip_levels(strip, from_e, from_w, e2, w2, fold, rows + 16)

    @pl.when(jnp.logical_not(on_top))
    def _():
        fold[...] = jnp.zeros_like(fold)

    scale = 2.0 / HALF
    last = (high - 8) // 8
    sub = _iota((8, 1), 0)
    for t in range(1, total // 8 - 1):
        a = 8 * t
        o = ext[1, a : a + 8, :]
        os = o * scale
        e = ext[3, a : a + 8, :]
        n = ext[4, a : a + 8, :]
        d = (ext[2, a : a + 8, :] - MID) * scale + os * (e + _lanes_right(e) + n + ext[4, a - 1 : a + 7, :])
        if t == last:
            d = d + jnp.where(sub == 7, fold[4:5, :], 0.0)
        coef[0, a : a + 8, :] = d
        coef[1, a : a + 8, :] = e * os * _lanes_left(o)
        coef[2, a : a + 8, :] = n * os * ext[1, a + 1 : a + 9, :]
    coef[2, 0:8, :] = jnp.zeros((8, wide), F32)

    outs = (t1, t2, t3, t4)
    sums = []
    own = r[0:8, :]
    square = own * own
    for t in range(1, rows // 8):
        own = r[8 * t : 8 * t + 8, :]
        square = square + own * own
    sums.append(square)
    for k in range(4):
        source = 0 if k == 0 else 4 + k
        square = cross = None
        tiles = range(2, total // 8 - 2) if k == 3 else range(1, total // 8 - 1)
        for t in tiles:
            a = 8 * t
            v = ext[source, a : a + 8, :]
            ce = coef[1, a : a + 8, :]
            new = (
                coef[0, a : a + 8, :] * v
                - ce * _lanes_left(v)
                - _lanes_right(ce * 1.0) * _lanes_right(v)
                - coef[2, a : a + 8, :] * ext[source, a + 1 : a + 9, :]
                - coef[2, a - 1 : a + 7, :] * ext[source, a - 1 : a + 7, :]
            )
            if t == last:
                new = new - jnp.where(sub == 7, fold[k : k + 1, :], 0.0)
            if k == 0:
                new = 0.5 * new
            else:
                new = new - ext[0 if k == 1 else 3 + k, a : a + 8, :]
            if k < 3:
                ext[5 + k, a : a + 8, :] = new
            if pad <= a < high:
                mine = new[:, :cols]
                outs[k][a - pad : a - pad + 8, :] = mine
                x = mine * v[:, :cols]
                cross = x if cross is None else cross + x
                if k < 3:
                    s = mine * mine
                    square = s if square is None else square + s
        sums.append(cross)
        if k < 3:
            sums.append(square)
    out = jnp.zeros((1, LANES), F32)
    for k, x in enumerate(sums):
        folded = x[:, :LANES] + x[:, LANES:]
        one = jnp.sum(jnp.sum(folded, axis=0, keepdims=True), axis=1, keepdims=True)
        out = jnp.where(lane == k, one, out)
    moments[...] = jnp.broadcast_to(out, moments.shape)


def basis(top, fields, from_n, from_s, from_e, from_w, strip, e2, w2, devices):
    rows, cols = fields[0].shape
    vmem = pl.BlockSpec(memory_space=pltpu.VMEM)
    out = jax.ShapeDtypeStruct((rows, cols), F32)
    return pl.pallas_call(
        _basis,
        in_specs=[pl.BlockSpec(memory_space=pltpu.SMEM)] + [vmem] * 12,
        out_specs=(vmem,) * 5,
        out_shape=(out,) * 4 + (jax.ShapeDtypeStruct((devices, LANES), F32),),
        scratch_shapes=[
            pltpu.VMEM((8, rows + 32, cols + LANES), F32),
            pltpu.VMEM((3, rows + 32, cols + LANES), F32),
            pltpu.VMEM((8, cols + LANES), F32),
        ],
        name="basis",
    )(top, *fields, from_n, from_s, from_e, from_w, strip, e2, w2)


def _combine(gathered, r, t1, t2, t3, t4, x_out, r_out):
    sums = jnp.sum(gathered[...], axis=0, keepdims=True)
    m = [sums[:, k : k + 1] for k in range(8)]
    nu = [m[0], m[1]]
    for k in range(1, 4):
        nu += [2.0 * m[2 * k] - m[0], 2.0 * m[2 * k + 1] - m[1]]
    gram = {}
    for i in range(4):
        for j in range(i, 5):
            if i == 0:
                gram[i, j] = nu[j]
            else:
                gram[i, j] = 0.5 * (nu[i + j] + nu[j - i])
            gram[j, i] = gram[i, j]

    def dot(a, b):
        total = None
        for i, p in enumerate(a):
            inner = None
            for j, q in enumerate(b):
                term = q * gram[i, j]
                inner = term if inner is None else inner + term
            inner = p * inner
            total = inner if total is None else total + inner
        return total

    def apply(v):
        n = len(v)
        out = [MID * x for x in v] + [None]
        for j, x in enumerate(v):
            if j == 0:
                up = HALF * x
            else:
                up = (0.5 * HALF) * x
                out[j - 1] = out[j - 1] + up
            out[j + 1] = up if out[j + 1] is None else out[j + 1] + up
        return out

    def add(a, s, b):
        out = []
        for i in range(max(len(a), len(b))):
            if i >= len(a):
                out.append(s * b[i])
            elif i >= len(b):
                out.append(a[i])
            else:
                out.append(a[i] + s * b[i])
        return out

    one = jnp.ones((1, 1), F32)
    solution_field, residual, direction = ([], [one], [one])
    norm_now = m[0]
    for iteration in range(ITERS):
        image = apply(direction)
        alpha = norm_now / dot(direction, image)
        solution_field = add(solution_field, alpha, direction)
        residual = add(residual, -alpha, image)
        if iteration + 1 < ITERS:
            norm_next = dot(residual, residual)
            direction = add(residual, norm_next / norm_now, direction)
            norm_now = norm_next
    basis_refs = (r, t1, t2, t3, t4)
    for start in range(0, r.shape[0], 8):
        span = pl.ds(start, 8)
        tiles = [ref[span, :] for ref in basis_refs]
        x = solution_field[0] * tiles[0]
        z = residual[0] * tiles[0]
        for k in range(1, 5):
            if k < 4:
                x = x + solution_field[k] * tiles[k]
            z = z + residual[k] * tiles[k]
        x_out[span, :] = x
        r_out[span, :] = z


def combine(gathered, r, t1, t2, t3, t4):
    vmem = pl.BlockSpec(memory_space=pltpu.VMEM)
    out = jax.ShapeDtypeStruct(r.shape, F32)
    return pl.pallas_call(
        _combine, in_specs=[vmem] * 6, out_specs=(vmem,) * 2, out_shape=(out, out), name="combine"
    )(gathered, r, t1, t2, t3, t4)


def local(right_side, diagonal, east_coef, north_coef, land_sea, fold_partner):
    cols = right_side.shape[1]
    lats, lons = (lax.axis_size(LAT), lax.axis_size(LON))
    devices = lats * lons
    top = (lax.axis_index(LAT) == lats - 1).astype(jnp.int32).reshape(1)
    fields = (right_side, land_sea, diagonal, east_coef, north_coef)

    def at(i, j):
        return i * lons + j % lons

    def top_row(x, partner):
        return lax.ppermute(x, LAT_LON, [(at(lats - 1, partner(j)), at(lats - 1, j)) for j in range(lons)])

    to_south, to_north = pack_rows(fields, fold_partner.reshape(1, cols))
    from_m = top_row(to_north, lambda j: lons - 1 - j)
    from_n = lax.ppermute(to_south, LAT, [(i + 1, i) for i in range(lats - 1)])
    from_s = lax.ppermute(to_north, LAT, [(i, i + 1) for i in range(lats - 1)])
    to_w, to_e, strip = pack_cols(top, fields, from_n, from_s, from_m, to_north)
    e2 = top_row(strip, lambda j: j + 2)
    w2 = top_row(strip, lambda j: j - 2)
    from_e = lax.ppermute(to_w, LON, [((j + 1) % lons, j) for j in range(lons)])
    from_w = lax.ppermute(to_e, LON, [(j, (j + 1) % lons) for j in range(lons)])
    t1, t2, t3, t4, moments = basis(
        top, fields, from_n, from_s, from_e, from_w, strip, e2, w2, devices
    )
    gathered = lax.all_to_all(moments, LAT_LON, 0, 0)
    return combine(gathered, right_side, t1, t2, t3, t4)


def solution(mesh):
    torus = Mesh(mesh.devices.reshape(2, 4, 2, 4, 2), ("lat_0", "lat_1", "lon_0", "lon_1", "lon_2"))
    placed = (P(LAT, LON), P(LAT, LON), P(LAT, LON), P(LAT, LON), P(LAT, LON), P(LON))
    return jax.shard_map(
        local, mesh=torus, in_specs=placed, out_specs=(P(LAT, LON), P(LAT, LON)), check_vma=False
    )
```

time: 250 us -> 59.2 us (0.24)
  blocking collectives: 145 us -> 33.3 us
  starting transfers between devices: 58.5 us -> 11.4 us
  between operations: 15.2 us -> 0.75 us
  local copies, waits for them, and re-layouts: 12.8 us -> 1.89 us
  Pallas kernels: 0 us -> 9 us
  waiting for transfers between devices: 11.5 us -> 2.51 us
  other arithmetic: 5.75 us -> 0 us
    psum x20 -> x0, blocking collectives: 145 us -> none  [over_axes(): return functools.reduce(lax.psum, axes, x)]
    ppermute x40 -> x7, starting transfers between devices: 58.5 us -> 11.4 us  [the longest x1 4.65 us: local(): from_s = lax.ppermute(to_north, LAT, [(i, i + 1) for i in range(lats - 1)])]
    all_to_all x0 -> x1, blocking collectives: none -> 33.3 us  [local(): gathered = lax.all_to_all(moments, LAT_LON, 0, 0)]
    gather x5 -> x0, local copies, waits for them, and re-layouts: 9.71 us -> none  [mirror_row(): return jnp.take(moving, local_cols, axis=0)]
    pallas_call x0 -> x4, Pallas kernels: none -> 9 us  [the longest x1 3.15 us: basis(): pl.pallas_call(_basis, in_specs=[pl.BlockSpec(memory_space=pltpu.SMEM)] +...]
    ppermute x40 -> x7, waiting for transfers between devices: 11.5 us -> 2.51 us  [the longest x1 1.4 us: local(): from_e = lax.ppermute(to_w, LON, [((j + 1) % lons, j) for j in range(lons)])]
    reduce_sum x4 -> x0, other arithmetic: 2.76 us -> none  [paired(): jnp.sum(residual * image)]
    slice x12 -> x0, local copies, waits for them, and re-layouts: 2.71 us -> none  [the longest x3 1.67 us: padded(): last = lax.slice_in_dim(x, length - width, length, axis=dim)]
  transfers between devices with their start and end apart: 40 -> 7, of which waited for: 15 -> 2; matrix products, arithmetic and copies ran while one was open for 2% -> 0% of each run, Pallas kernels for 0% -> 0%
where the time goes in v1:
time: 59.2 us; the launch traced here: 58.9 us
  blocking collectives  33.3 us (56%)
  starting transfers between devices  11.4 us (19%)
  Pallas kernels  9 us (15%)
  waiting for transfers between devices  2.51 us (4%)
  local copies, waits for them, and re-layouts  1.89 us (3%)
  between operations  0.75 us (1%)
    all_to_all x1, blocking collectives, local(): gathered = lax.all_to_all(moments, LAT_LON, 0, 0)  33.3 us
    ppermute x1, starting transfers between devices, local(): from_s = lax.ppermute(to_north, LAT, [(i, i + 1) for i in range(lats - 1)])  4.65 us
    pallas_call x1, Pallas kernels, basis(): pl.pallas_call(_basis, in_specs=[pl.BlockSpec(memory_space=pltpu.SMEM)] +...  3.15 us
    pallas_call x1, Pallas kernels, combine(): pl.pallas_call(_combine, in_specs=[vmem] * 6, out_specs=(vmem,) * 2, out_...  2.24 us
    pallas_call x1, Pallas kernels, pack_cols(): pl.pallas_call(_pack_cols, in_specs=[pl.BlockSpec(memory_space=pltpu.SMEM...  2.14 us
    ppermute x3, starting transfers between devices, top_row(): lax.ppermute(x, LAT_LON, [(at(lats - 1, partner(j)), at(lats - 1, j)) for...  1.98 us
    unnamed x14, local copies, waits for them, and re-layouts  1.89 us
    ppermute x1, starting transfers between devices, local(): from_e = lax.ppermute(to_w, LON, [((j + 1) % lons, j) for j in range(lons)])  1.85 us
  transfers between devices with their start and end apart: 7, of which 2 were waited for; matrix products, arithmetic and copies ran while one was open for 0% of the time, Pallas kernels for 0%

profile of v1, /device:TPU:1, one launch (start us, length us, event | category | flops | bytes accessed | tf_op | source)
XLA Modules:
  0.0 58.9 jit_solution(8341553867184764918)
XLA Ops:
  0.6 1.5 %pack_rows.1 = (f32[24,256]{1,0:T(8,128)}, f32[24,256]{1,0:T(8,128)}) custom-call(f32[128,256]{1,0:T(8,128)} %r.5, s32[128,256]{1,0:T(8,128)} %oc.3, f32[128,256]{1,0:T(8,128)} %dg.3, f32[128,256]{1,0:T(8,128)} %ea.3, f32[128,256]{1,0:T(8,128)} %no.3, f32[128,256]{1,0:T(8,128)} %r.5, s32[128,256]{1,0:T(8,128)} %oc.3, f32[128,256]{1,0:T(8,128)} %dg.3, ...), custom_call_target="tpu_custom_call" | custom-call | tf_op jit(solution)/shard_map/pack_rows/pallas_call | solution.py:46
  2.1 1.3 %collective-permute-start = (f32[24,256]{1,0:T(8,128)}, f32[24,256]{1,0:T(8,128)S(1)}, u32[]{:S(2)}, u32[]{:S(2)}) collective-permute-start(f32[24,256]{1,0:T(8,128)} %get-tuple-element.12), channel_id=1, source_target_pairs={{16,0},{32,16},{48,32},{64,48},{80,64},{96,80},{112,96},{17,1},{33... | collective-permute-start | bytes 73736 | tf_op jit(solution)/shard_map/ppermute | solution.py:449
  3.4 0.7 %collective-permute-start.2 = (f32[24,256]{1,0:T(8,128)}, f32[24,256]{1,0:T(8,128)S(1)}, u32[]{:S(2)}, u32[]{:S(2)}) collective-permute-start(f32[24,256]{1,0:T(8,128)} %get-tuple-element.13.own_top), channel_id=1, source_target_pairs={{127,112},{126,113},{125,114},{124,115},{123,116},{122,117},{121,1... | collective-permute-start | bytes 73736 | tf_op jit(solution)/shard_map/ppermute | solution.py:445
  4.1 4.6 %collective-permute-start.1 = (f32[24,256]{1,0:T(8,128)}, f32[24,256]{1,0:T(8,128)S(1)}, u32[]{:S(2)}, u32[]{:S(2)}) collective-permute-start(f32[24,256]{1,0:T(8,128)} %get-tuple-element.13.own_top), channel_id=1, source_target_pairs={{0,16},{16,32},{32,48},{48,64},{64,80},{80,96},{96,112},{1,17},{17... | collective-permute-start | bytes 73736 | tf_op jit(solution)/shard_map/ppermute | solution.py:450
  8.7 0.0 collective-permute-done.from_n
  8.7 0.0 collective-permute-done.2.from_m
  8.8 0.0 copy-start.6
  8.8 1.1 %collective-permute-done.1.from_s = f32[24,256]{1,0:T(8,128)S(1)} collective-permute-done((f32[24,256]{1,0:T(8,128)}, f32[24,256]{1,0:T(8,128)S(1)}, u32[]{:S(2)}, u32[]{:S(2)}) %collective-permute-start.1) | collective-permute-done | bytes 24608 | tf_op jit(solution)/shard_map/ppermute | solution.py:450
  9.9 0.0 copy-done.2
  9.9 0.6 %copy-done.3 = f32[24,256]{1,0:T(8,128)} copy-done((f32[24,256]{1,0:T(8,128)}, f32[24,256]{1,0:T(8,128)S(1)}, u32[]{:S(2)}) %copy-start.3) | copy-done | bytes 24600
  10.5 2.1 %pack_cols.1 = (f32[240,128]{1,0:T(8,128)}, f32[240,128]{1,0:T(8,128)}, f32[48,256]{1,0:T(8,128)}) custom-call(s32[1]{0:T(128)} %bitcast.top, f32[128,256]{1,0:T(8,128)} %r.5, s32[128,256]{1,0:T(8,128)} %oc.3, f32[128,256]{1,0:T(8,128)} %dg.3, f32[128,256]{1,0:T(8,128)} %ea.3, f32[128,256]{1,0:T(8,128)} %no.3, f32[24,256]{1,0:T(8,128)} %copy-done.2, ...), custom_call_target="tpu_custom_call" | custom-call | tf_op jit(solution)/shard_map/pack_cols/pallas_call | solution.py:133
  12.6 1.9 %collective-permute-start.3 = (f32[240,128]{1,0:T(8,128)}, f32[240,128]{1,0:T(8,128)S(1)}, u32[]{:S(2)}, u32[]{:S(2)}) collective-permute-start(f32[240,128]{1,0:T(8,128)} %get-tuple-element.14), channel_id=1, source_target_pairs={{1,0},{2,1},{3,2},{4,3},{5,4},{6,5},{7,6},{8,7},{9,8},{10,9},{11,1... | collective-permute-start | bytes 368648 | tf_op jit(solution)/shard_map/ppermute | solution.py:454
  14.5 1.6 %collective-permute-start.4 = (f32[240,128]{1,0:T(8,128)}, f32[240,128]{1,0:T(8,128)S(1)}, u32[]{:S(2)}, u32[]{:S(2)}) collective-permute-start(f32[240,128]{1,0:T(8,128)} %get-tuple-element.15), channel_id=1, source_target_pairs={{0,1},{1,2},{2,3},{3,4},{4,5},{5,6},{6,7},{7,8},{8,9},{9,10},{10,1... | collective-permute-start | bytes 368648 | tf_op jit(solution)/shard_map/ppermute | solution.py:455
  16.1 0.7 %collective-permute-start.6 = (f32[48,256]{1,0:T(8,128)}, f32[48,256]{1,0:T(8,128)S(1)}, u32[]{:S(2)}, u32[]{:S(2)}) collective-permute-start(f32[48,256]{1,0:T(8,128)} %get-tuple-element.16.strip), channel_id=1, source_target_pairs={{126,112},{127,113},{112,114},{113,115},{114,116},{115,117},{116,1... | collective-permute-start | bytes 147464 | tf_op jit(solution)/shard_map/ppermute | solution.py:445
  16.7 0.7 %collective-permute-start.5 = (f32[48,256]{1,0:T(8,128)}, f32[48,256]{1,0:T(8,128)S(1)}, u32[]{:S(2)}, u32[]{:S(2)}) collective-permute-start(f32[48,256]{1,0:T(8,128)} %get-tuple-element.16.strip), channel_id=1, source_target_pairs={{114,112},{115,113},{116,114},{117,115},{118,116},{119,117},{120,1... | collective-permute-start | bytes 147464 | tf_op jit(solution)/shard_map/ppermute | solution.py:445
  17.4 0.0 collective-permute-done.6.w2
  17.4 0.0 collective-permute-done.5.e2
  17.5 1.4 %collective-permute-done.3.from_e = f32[240,128]{1,0:T(8,128)S(1)} collective-permute-done((f32[240,128]{1,0:T(8,128)}, f32[240,128]{1,0:T(8,128)S(1)}, u32[]{:S(2)}, u32[]{:S(2)}) %collective-permute-start.3) | collective-permute-done | bytes 122912 | tf_op jit(solution)/shard_map/ppermute | solution.py:454
  18.9 0.0 collective-permute-done.4.from_w
  18.9 0.6 %copy-done = f32[240,128]{1,0:T(8,128)} copy-done((f32[240,128]{1,0:T(8,128)}, f32[240,128]{1,0:T(8,128)S(1)}, u32[]{:S(2)}) %copy-start) | copy-done | bytes 122904
  19.5 0.6 %copy-done.1 = f32[240,128]{1,0:T(8,128)} copy-done((f32[240,128]{1,0:T(8,128)}, f32[240,128]{1,0:T(8,128)S(1)}, u32[]{:S(2)}) %copy-start.1) | copy-done | bytes 122904
  20.2 3.1 %basis.1 = (f32[128,256]{1,0:T(8,128)}, f32[128,256]{1,0:T(8,128)}, f32[128,256]{1,0:T(8,128)}, f32[128,256]{1,0:T(8,128)}, f32[128,128]{1,0:T(8,128)}) custom-call(s32[1]{0:T(128)} %bitcast.top, f32[128,256]{1,0:T(8,128)} %r.5, s32[128,256]{1,0:T(8,128)} %oc.3, f32[128,256]{1,0:T(8,128)} %dg.3, f32[128,256]{1,0:T(8,128)} %ea.3, f32[128,256]{1,0:T(8,128)} %no.3, ...), custom_call_target="tpu_custom_call" | custom-call | tf_op jit(solution)/shard_map/basis/pallas_call | solution.py:337
  23.3 33.3 %all_to_all.11 = f32[128,1,128]{2,1,0:T(1,128)} all-to-all(f32[128,1,128]{2,1,0:T(1,128)} %bitcast.7), channel_id=1, replica_groups=mesh['lat_0'=2,'lat_1'=4,'lon_0'=2,'lon_1'=4,'lon_2'=2] {'lat_0','lat_1'..., dimensions={0} | all-to-all | bytes 131072 | tf_op jit(solution)/shard_map/all_to_all | solution.py:459
  56.6 2.2 %combine.1 = (f32[128,256]{1,0:T(8,128)}, f32[128,256]{1,0:T(8,128)}) custom-call(f32[128,128]{1,0:T(8,128)} %bitcast.6, f32[128,256]{1,0:T(8,128)} %r.5, f32[128,256]{1,0:T(8,128)} %get-tuple-element.18.t1, f32[128,256]{1,0:T(8,128)} %get-tuple-element.19.t2, f32[128,256]{1,0:T(8,128)} %get-tuple-element.20.t3, f32[128,256]{1,0:T(8,128)} %get-tuple-element.21.t4), custom_call_target="tpu_custom_call" | custom-call | tf_op jit(solution)/shard_map/combine/pallas_call | solution.py:429
  (9 shorter events, 0.0 us)
Async XLA Ops:
  2.1 6.6 %collective-permute-start = (f32[24,256]{1,0:T(8,128)}, f32[24,256]{1,0:T(8,128)S(1)}, u32[]{:S(2)}, u32[]{:S(2)}) collective-permute-start(f32[24,256]{1,0:T(8,128)} %get-tuple-element.12), channel_id=1, source_target_pairs={{16,0},{32,16},{48,32},{64,48},{80,64},{96,80},{112,96},{17,1},{33... | collective-permute-start | bytes 73736 | tf_op jit(solution)/shard_map/ppermute | solution.py:449
  3.4 5.4 %collective-permute-start.2 = (f32[24,256]{1,0:T(8,128)}, f32[24,256]{1,0:T(8,128)S(1)}, u32[]{:S(2)}, u32[]{:S(2)}) collective-permute-start(f32[24,256]{1,0:T(8,128)} %get-tuple-element.13.own_top), channel_id=1, source_target_pairs={{127,112},{126,113},{125,114},{124,115},{123,116},{122,117},{121,1... | collective-permute-start | bytes 73736 | tf_op jit(solution)/shard_map/ppermute | solution.py:445
  4.1 5.8 %collective-permute-start.1 = (f32[24,256]{1,0:T(8,128)}, f32[24,256]{1,0:T(8,128)S(1)}, u32[]{:S(2)}, u32[]{:S(2)}) collective-permute-start(f32[24,256]{1,0:T(8,128)} %get-tuple-element.13.own_top), channel_id=1, source_target_pairs={{0,16},{16,32},{32,48},{48,64},{64,80},{80,96},{96,112},{1,17},{17... | collective-permute-start | bytes 73736 | tf_op jit(solution)/shard_map/ppermute | solution.py:450
  8.7 1.1 %copy-start.2 = (f32[24,256]{1,0:T(8,128)}, f32[24,256]{1,0:T(8,128)S(1)}, u32[]{:S(2)}) copy-start(f32[24,256]{1,0:T(8,128)S(1)} %collective-permute-done.from_n) | copy-start | bytes 73732
  8.8 1.1 %copy-start.6 = (f32[24,256]{1,0:T(8,128)}, f32[24,256]{1,0:T(8,128)S(1)}, u32[]{:S(2)}) copy-start(f32[24,256]{1,0:T(8,128)S(1)} %collective-permute-done.2.from_m) | copy-start | bytes 73732
  9.9 0.6 %copy-start.3 = (f32[24,256]{1,0:T(8,128)}, f32[24,256]{1,0:T(8,128)S(1)}, u32[]{:S(2)}) copy-start(f32[24,256]{1,0:T(8,128)S(1)} %collective-permute-done.1.from_s) | copy-start | bytes 73732
  12.6 6.3 %collective-permute-start.3 = (f32[240,128]{1,0:T(8,128)}, f32[240,128]{1,0:T(8,128)S(1)}, u32[]{:S(2)}, u32[]{:S(2)}) collective-permute-start(f32[240,128]{1,0:T(8,128)} %get-tuple-element.14), channel_id=1, source_target_pairs={{1,0},{2,1},{3,2},{4,3},{5,4},{6,5},{7,6},{8,7},{9,8},{10,9},{11,1... | collective-permute-start | bytes 368648 | tf_op jit(solution)/shard_map/ppermute | solution.py:454
  14.5 4.4 %collective-permute-start.4 = (f32[240,128]{1,0:T(8,128)}, f32[240,128]{1,0:T(8,128)S(1)}, u32[]{:S(2)}, u32[]{:S(2)}) collective-permute-start(f32[240,128]{1,0:T(8,128)} %get-tuple-element.15), channel_id=1, source_target_pairs={{0,1},{1,2},{2,3},{3,4},{4,5},{5,6},{6,7},{7,8},{8,9},{9,10},{10,1... | collective-permute-start | bytes 368648 | tf_op jit(solution)/shard_map/ppermute | solution.py:455
  16.1 1.3 %collective-permute-start.6 = (f32[48,256]{1,0:T(8,128)}, f32[48,256]{1,0:T(8,128)S(1)}, u32[]{:S(2)}, u32[]{:S(2)}) collective-permute-start(f32[48,256]{1,0:T(8,128)} %get-tuple-element.16.strip), channel_id=1, source_target_pairs={{126,112},{127,113},{112,114},{113,115},{114,116},{115,117},{116,1... | collective-permute-start | bytes 147464 | tf_op jit(solution)/shard_map/ppermute | solution.py:445
  16.7 0.7 %collective-permute-start.5 = (f32[48,256]{1,0:T(8,128)}, f32[48,256]{1,0:T(8,128)S(1)}, u32[]{:S(2)}, u32[]{:S(2)}) collective-permute-start(f32[48,256]{1,0:T(8,128)} %get-tuple-element.16.strip), channel_id=1, source_target_pairs={{114,112},{115,113},{116,114},{117,115},{118,116},{119,117},{120,1... | collective-permute-start | bytes 147464 | tf_op jit(solution)/shard_map/ppermute | solution.py:445
  17.4 1.4 %copy-start.4 = (f32[48,256]{1,0:T(8,128)}, f32[48,256]{1,0:T(8,128)S(1)}, u32[]{:S(2)}) copy-start(f32[48,256]{1,0:T(8,128)S(1)} %collective-permute-done.6.w2) | copy-start | bytes 147460
  17.4 1.4 %copy-start.5 = (f32[48,256]{1,0:T(8,128)}, f32[48,256]{1,0:T(8,128)S(1)}, u32[]{:S(2)}) copy-start(f32[48,256]{1,0:T(8,128)S(1)} %collective-permute-done.5.e2) | copy-start | bytes 147460
  18.9 0.6 %copy-start = (f32[240,128]{1,0:T(8,128)}, f32[240,128]{1,0:T(8,128)S(1)}, u32[]{:S(2)}) copy-start(f32[240,128]{1,0:T(8,128)S(1)} %collective-permute-done.3.from_e) | copy-start | bytes 368644
  19.5 0.6 %copy-start.1 = (f32[240,128]{1,0:T(8,128)}, f32[240,128]{1,0:T(8,128)S(1)}, u32[]{:S(2)}) copy-start(f32[240,128]{1,0:T(8,128)S(1)} %collective-permute-done.4.from_w) | copy-start | bytes 368644

commit v2 on v1

--- a/solution.py
+++ b/solution.py
@@ -28,17 +28,19 @@
     return jnp.concatenate(parts, axis=axis)
 
 
-def _pack_rows(*refs):
-    bottoms, tops, (partner, south_out, north_out) = (refs[:5], refs[5:10], refs[10:])
-    south_out[...] = jnp.zeros_like(south_out)
-    north_out[...] = jnp.zeros_like(north_out)
+def _pack_rows(flags, *refs):
+    bottoms, tops, (partner, first, second) = (refs[:5], refs[5:10], refs[10:])
+    even = flags[1] == 0
     for f in range(5):
-        south_out[W * f : W * f + W, :] = bottoms[f][0:W, :].astype(F32)
-        north_out[W * f : W * f + W, :] = tops[f][8 - W : 8, :].astype(F32)
-    north_out[20:21, :] = partner[...].astype(F32)
-
-
-def pack_rows(fields, partner):
+        low = bottoms[f][0:W, :].astype(F32)
+        high = tops[f][8 - W : 8, :].astype(F32)
+        first[W * f : W * f + W, :] = jnp.where(even, high, low)
+        second[W * f : W * f + W, :] = jnp.where(even, low, high)
+    first[20:24, :] = jnp.zeros((4, first.shape[1]), F32)
+    second[20:24, :] = jnp.broadcast_to(partner[...].astype(F32), (4, first.shape[1]))
+
+
+def pack_rows(flags, fields, partner):
     rows, cols = fields[0].shape
     low = pl.BlockSpec((8, cols), lambda i: (0, 0))
     high = pl.BlockSpec((8, cols), lambda i: (rows // 8 - 1, 0))
@@ -46,11 +48,14 @@
     return pl.pallas_call(
         _pack_rows,
         grid=(1,),
-        in_specs=[low] * 5 + [high] * 5 + [pl.BlockSpec((1, cols), lambda i: (0, 0))],
+        in_specs=[pl.BlockSpec(memory_space=pltpu.SMEM)]
+        + [low] * 5
+        + [high] * 5
+        + [pl.BlockSpec((1, cols), lambda i: (0, 0))],
         out_specs=(pl.BlockSpec((24, cols), lambda i: (0, 0)),) * 2,
         out_shape=(out, out),
         name="pack_rows",
-    )(*fields, *fields, partner)
+    )(flags, *fields, *fields, partner)
 
 
 def _pick(source, index):
@@ -64,9 +69,16 @@
     return _cat(outs, 1)
 
 
-def _pack_cols(top, r, oc, dg, ea, no, from_n, from_s, from_m, own_top, to_w, to_e, strip):
+def _pack_cols(flags, r, oc, dg, ea, no, first, second, own_top, to_chip, to_far, strip):
     rows = r.shape[0]
     lane = _iota((1, LANES), 1)
+    on_top = flags[0] == 1
+    row_even = flags[1] == 0
+    col_even = flags[2] == 0
+
+    def store(at, count, west, east):
+        to_chip[at : at + count, :] = jnp.where(col_even, east, west)
+        to_far[at : at + count, :] = jnp.where(col_even, west, east)
 
     def packed(pieces):
         west = east = None
@@ -88,24 +100,23 @@
         west, east = packed(
             [(x[span, :LANES].astype(F32), x[span, LANES:].astype(F32)) for x in (r, oc, dg, ea, no)]
         )
-        to_w[pl.ds(8 + start, 32), :] = west
-        to_e[pl.ds(8 + start, 32), :] = east
-    for src, base, blank in ((from_s, 4, 0), (from_n, 8 + rows, 12 + rows)):
-        west, east = packed(
-            [(src[W * f : W * f + W, :LANES], src[W * f : W * f + W, LANES:]) for f in range(5)]
-        )
-        to_w[base : base + W, :] = west
-        to_e[base : base + W, :] = east
-        to_w[blank : blank + W, :] = zero
-        to_e[blank : blank + W, :] = zero
-
-    @pl.when(top[0] == 1)
+        store(8 + start, 32, west, east)
+    for base, blank, choose in ((4, 0, row_even), (8 + rows, 12 + rows, jnp.logical_not(row_even))):
+        pieces = []
+        for f in range(5):
+            x = jnp.where(choose, second[W * f : W * f + W, :], first[W * f : W * f + W, :])
+            pieces.append((x[:, :LANES], x[:, LANES:]))
+        west, east = packed(pieces)
+        store(base, W, west, east)
+        store(blank, W, zero, zero)
+
+    @pl.when(on_top)
     def _():
         for f in range(5):
             strip[8 * f : 8 * f + W, :] = own_top[W * f : W * f + W, :]
-            strip[8 * f + W : 8 * f + 8, :] = from_m[W * f : W * f + W, :]
+            strip[8 * f + W : 8 * f + 8, :] = second[W * f : W * f + W, :]
         strip[40:48, :] = jnp.zeros((8, 2 * LANES), F32)
-        own_partner, far_partner = (own_top[20:21, :], from_m[20:21, :])
+        own_partner, far_partner = (own_top[20:21, :], second[20:21, :])
         strip[40:41, :] = own_partner
         strip[41:42, :] = far_partner
         row = _iota((8, 1), 0)
@@ -122,21 +133,21 @@
     base = rows + 16
     for half in range(2):
         part = strip[:, half * LANES : (half + 1) * LANES]
-        to_w[base + STRIP * half : base + STRIP * (half + 1), :] = part
-        to_e[base + STRIP * half : base + STRIP * (half + 1), :] = part
-
-
-def pack_cols(top, fields, from_n, from_s, from_m, own_top):
+        to_chip[base + STRIP * half : base + STRIP * (half + 1), :] = part
+        to_far[base + STRIP * half : base + STRIP * (half + 1), :] = part
+
+
+def pack_cols(flags, fields, first, second, own_top):
     rows, cols = fields[0].shape
     message = jax.ShapeDtypeStruct((rows + 16 + 2 * STRIP, LANES), F32)
     vmem = pl.BlockSpec(memory_space=pltpu.VMEM)
     return pl.pallas_call(
         _pack_cols,
-        in_specs=[pl.BlockSpec(memory_space=pltpu.SMEM)] + [vmem] * 9,
+        in_specs=[pl.BlockSpec(memory_space=pltpu.SMEM)] + [vmem] * 8,
         out_specs=(vmem,) * 3,
         out_shape=(message, message, jax.ShapeDtypeStruct((STRIP, cols), F32)),
         name="pack_cols",
-    )(top, *fields, from_n, from_s, from_m, own_top)
+    )(flags, *fields, first, second, own_top)
 
 
 def _lanes_left(x):
@@ -147,15 +158,13 @@
     return pltpu.roll(x, 1, 1)
 
 
-def _strip_levels(strip, from_e, from_w, e2, w2, fold, base):
+def _strip_levels(strip, sides, fold):
     row = _iota((8, 1), 0)
     lane = _iota((1, LANES), 1)
     near = row < 4
 
-    def far(ref, at, count):
-        return _cat(
-            [ref[base + at : base + at + count, :], ref[base + STRIP + at : base + STRIP + at + count, :]], 1
-        )
+    def far(side, at, count):
+        return _cat([sides[side, at : at + count, :], sides[side, STRIP + at : STRIP + at + count, :]], 1)
 
     def assembled(mine, east, west, east2, west2):
         left = jnp.where(near, west, east)
@@ -169,9 +178,7 @@
 
     def field(f):
         s = 8 * f
-        return assembled(
-            strip[s : s + 8, :], far(from_e, s, 8), far(from_w, s, 8), e2[s : s + 8, :], w2[s : s + 8, :]
-        )
+        return assembled(strip[s : s + 8, :], *(far(side, s, 8) for side in range(4)))
 
     def pair(at):
         def one(a, b):
@@ -179,10 +186,7 @@
 
         return assembled(
             one(strip[at : at + 1, :], strip[at + 1 : at + 2, :]),
-            one(far(from_e, at, 1), far(from_e, at + 1, 1)),
-            one(far(from_w, at, 1), far(from_w, at + 1, 1)),
-            one(e2[at : at + 1, :], e2[at + 1 : at + 2, :]),
-            one(w2[at : at + 1, :], w2[at + 1 : at + 2, :]),
+            *(one(far(side, at, 1), far(side, at + 1, 1)) for side in range(4)),
         )
 
     r, oc, dg, ea, no = [field(f) for f in range(5)]
@@ -228,26 +232,30 @@
         neighbour = _cat([*picked, jnp.zeros((8, LANES), F32)], 1)
 
 
-def _basis(top, r, oc, dg, ea, no, from_n, from_s, from_e, from_w, strip, e2, w2, t1, t2, t3, t4, moments, ext, coef, fold):
+def _basis(flags, r, oc, dg, ea, no, first, second, chip, far, far2, chip2, strip, t1, t2, t3, t4, moments, ext, coef, fold, sides):
     rows, cols = r.shape
     pad = 16
     high = rows + pad
     wide = cols + LANES
     lane = _iota((1, LANES), 1)
     total = rows + 2 * pad
-    on_top = top[0] == 1
+    on_top = flags[0] == 1
+    row_even = flags[1] == 0
+    col_even = flags[2] == 0
     for f, own in enumerate((r, oc, dg, ea, no)):
         ext[f, 0 : pad, :cols] = jnp.zeros((pad, cols), F32)
         ext[f, high : high + pad, :cols] = jnp.zeros((pad, cols), F32)
         ext[f, pad:high, :cols] = own[...].astype(F32)
-        ext[f, pad - W : pad, :cols] = from_s[W * f : W * f + W, :]
-        ext[f, high : high + W, :cols] = from_n[W * f : W * f + W, :]
+        one, two = (first[W * f : W * f + W, :], second[W * f : W * f + W, :])
+        ext[f, pad - W : pad, :cols] = jnp.where(row_even, two, one)
+        ext[f, high : high + W, :cols] = jnp.where(row_even, one, two)
         ext[f, 0:8, cols:] = jnp.zeros((8, LANES), F32)
         ext[f, total - 8 : total, cols:] = jnp.zeros((8, LANES), F32)
-        east = from_e[0 : rows + 16, :]
+        east = jnp.where(col_even, chip[0 : rows + 16, :], far[0 : rows + 16, :])
         if f:
             east = pltpu.roll(east, LANES - W * f, 1)
-        west = pltpu.roll(from_w[0 : rows + 16, :], LANES - W - W * f, 1)
+        west = jnp.where(col_even, far[0 : rows + 16, :], chip[0 : rows + 16, :])
+        west = pltpu.roll(west, LANES - W - W * f, 1)
         halo = jnp.where(lane < W, east, jnp.where(lane >= LANES - W, west, 0.0))
         ext[f, 8 : 8 + rows + 16, cols:] = halo
     for k in (5, 6, 7):
@@ -257,7 +265,12 @@
     @pl.when(on_top)
     def _():
         ext[4, high - 1 : high, :] = jnp.zeros((1, wide), F32)
-        _strip_levels(strip, from_e, from_w, e2, w2, fold, rows + 16)
+        tail = slice(rows + 16, rows + 16 + 2 * STRIP)
+        sides[0] = jnp.where(col_even, chip[tail, :], far[tail, :])
+        sides[1] = jnp.where(col_even, far[tail, :], chip[tail, :])
+        sides[2] = jnp.where(col_even, chip2[tail, :], far2[tail, :])
+        sides[3] = jnp.where(col_even, far2[tail, :], chip2[tail, :])
+        _strip_levels(strip, sides, fold)
 
     @pl.when(jnp.logical_not(on_top))
     def _():
@@ -330,7 +343,7 @@
     moments[...] = jnp.broadcast_to(out, moments.shape)
 
 
-def basis(top, fields, from_n, from_s, from_e, from_w, strip, e2, w2, devices):
+def basis(flags, fields, first, second, chip, far, far2, chip2, strip, devices):
     rows, cols = fields[0].shape
     vmem = pl.BlockSpec(memory_space=pltpu.VMEM)
     out = jax.ShapeDtypeStruct((rows, cols), F32)
@@ -343,9 +356,10 @@
             pltpu.VMEM((8, rows + 32, cols + LANES), F32),
             pltpu.VMEM((3, rows + 32, cols + LANES), F32),
             pltpu.VMEM((8, cols + LANES), F32),
+            pltpu.VMEM((4, 2 * STRIP, LANES), F32),
         ],
         name="basis",
-    )(top, *fields, from_n, from_s, from_e, from_w, strip, e2, w2)
+    )(flags, *fields, first, second, chip, far, far2, chip2, strip)
 
 
 def _combine(gathered, r, t1, t2, t3, t4, x_out, r_out):
@@ -435,27 +449,42 @@
     cols = right_side.shape[1]
     lats, lons = (lax.axis_size(LAT), lax.axis_size(LON))
     devices = lats * lons
-    top = (lax.axis_index(LAT) == lats - 1).astype(jnp.int32).reshape(1)
+    lat, lon = (lax.axis_index(LAT), lax.axis_index(LON))
+    flags = jnp.stack([(lat == lats - 1).astype(jnp.int32), lat % 2, lon % 2])
     fields = (right_side, land_sea, diagonal, east_coef, north_coef)
 
-    def at(i, j):
-        return i * lons + j % lons
-
-    def top_row(x, partner):
-        return lax.ppermute(x, LAT_LON, [(at(lats - 1, partner(j)), at(lats - 1, j)) for j in range(lons)])
-
-    to_south, to_north = pack_rows(fields, fold_partner.reshape(1, cols))
-    from_m = top_row(to_north, lambda j: lons - 1 - j)
-    from_n = lax.ppermute(to_south, LAT, [(i + 1, i) for i in range(lats - 1)])
-    from_s = lax.ppermute(to_north, LAT, [(i, i + 1) for i in range(lats - 1)])
-    to_w, to_e, strip = pack_cols(top, fields, from_n, from_s, from_m, to_north)
-    e2 = top_row(strip, lambda j: j + 2)
-    w2 = top_row(strip, lambda j: j - 2)
-    from_e = lax.ppermute(to_w, LON, [((j + 1) % lons, j) for j in range(lons)])
-    from_w = lax.ppermute(to_e, LON, [(j, (j + 1) % lons) for j in range(lons)])
-    t1, t2, t3, t4, moments = basis(
-        top, fields, from_n, from_s, from_e, from_w, strip, e2, w2, devices
-    )
+    def swap(x, partner, rows=range(lats)):
+        pairs = []
+        for i in rows:
+            for j in range(lons):
+                there = partner(i, j)
+                if there is not None:
+                    pairs.append((i * lons + j, there[0] * lons + there[1] % lons))
+        return lax.ppermute(x, LAT_LON, pairs)
+
+    def second_row(i, j):
+        if i == lats - 1:
+            return (i, lons - 1 - j)
+        if i == 0:
+            return None
+        return (i + 1 if i % 2 else i - 1, j)
+
+    def off_chip(i, j):
+        return (i, j + 1 if j % 2 else j - 1)
+
+    def on_chip(i, j):
+        return (i, j ^ 1)
+
+    top = (lats - 1,)
+    to_first, to_second = pack_rows(flags, fields, fold_partner.reshape(1, cols))
+    first = swap(to_first, lambda i, j: (i ^ 1, j))
+    second = swap(to_second, second_row)
+    to_chip, to_far, strip = pack_cols(flags, fields, first, second, to_second)
+    chip = swap(to_chip, on_chip)
+    far = swap(to_far, off_chip)
+    far2 = swap(chip, off_chip, top)
+    chip2 = swap(far, on_chip, top)
+    t1, t2, t3, t4, moments = basis(flags, fields, first, second, chip, far, far2, chip2, strip, devices)
     gathered = lax.all_to_all(moments, LAT_LON, 0, 0)
     return combine(gathered, right_side, t1, t2, t3, t4)
 

time: 59.2 us -> 52.4 us (0.89)
  blocking collectives: 33.3 us -> 29.2 us
  starting transfers between devices: 11.4 us -> 7.66 us
  other arithmetic: 0 us -> 0.62 us
    all_to_all x1, blocking collectives: 33.3 us -> 29.2 us  [local(): gathered = lax.all_to_all(moments, LAT_LON, 0, 0)]
    ppermute x7 -> x6, starting transfers between devices: 11.4 us -> 7.66 us  [swap(): return lax.ppermute(x, LAT_LON, pairs)]
    another operation x0 -> x1, other arithmetic: none -> 0.62 us  [local(): flags = jnp.stack([(lat == lats - 1).astype(jnp.int32), lat % 2, lon % 2])]
    ppermute x7 -> x6, waiting for transfers between devices: 2.51 us -> 2.92 us  [swap(): return lax.ppermute(x, LAT_LON, pairs)]
    unnamed x14 -> x12, local copies, waits for them, and re-layouts: 1.89 us -> 1.86 us
  transfers between devices with their start and end apart: 7 -> 6, of which waited for: 2 -> 2; matrix products, arithmetic and copies ran while one was open for 0% -> 0% of each run, Pallas kernels for 0% -> 0%
where the time goes in v2:
time: 52.4 us; the launch traced here: 52.1 us
  blocking collectives  29.2 us (56%)
  Pallas kernels  9.03 us (17%)
  starting transfers between devices  7.66 us (15%)
  waiting for transfers between devices  2.92 us (6%)
  local copies, waits for them, and re-layouts  1.86 us (4%)
  between operations  0.74 us (1%)
  other arithmetic  0.62 us (1%)
    all_to_all x1, blocking collectives, local(): gathered = lax.all_to_all(moments, LAT_LON, 0, 0)  29.2 us
    ppermute x6, starting transfers between devices, swap(): return lax.ppermute(x, LAT_LON, pairs)  7.66 us
    pallas_call x1, Pallas kernels, basis(): pl.pallas_call(_basis, in_specs=[pl.BlockSpec(memory_space=pltpu.SMEM)] +...  3.16 us
    ppermute x6, waiting for transfers between devices, swap(): return lax.ppermute(x, LAT_LON, pairs)  2.92 us
    pallas_call x1, Pallas kernels, combine(): pl.pallas_call(_combine, in_specs=[vmem] * 6, out_specs=(vmem,) * 2, out_...  2.24 us
    pallas_call x1, Pallas kernels, pack_cols(): pl.pallas_call(_pack_cols, in_specs=[pl.BlockSpec(memory_space=pltpu.SMEM...  2.14 us
    unnamed x12, local copies, waits for them, and re-layouts  1.86 us
    pallas_call x1, Pallas kernels, pack_rows(): pl.pallas_call(_pack_rows, grid=(1,), in_specs=[pl.BlockSpec(memory_space...  1.48 us
  transfers between devices with their start and end apart: 6, of which 2 were waited for; matrix products, arithmetic and copies ran while one was open for 0% of the time, Pallas kernels for 0%

profile of v2, /device:TPU:1, one launch (start us, length us, event | category | flops | bytes accessed | tf_op | source)
XLA Modules:
  0.0 52.1 jit_solution(5040115230554090802)
XLA Ops:
  0.7 0.6 %pad_add_fusion.flags = s32[3]{0:T(128)} fusion(s32[1]{0:T(128)} %bitcast.2, s32[1]{0:T(128)} %bitcast.1, s32[1]{0:T(128)} %bitcast), kind=kLoop, calls=%fused_computation | loop fusion | flops 6 | bytes 24 | tf_op jit(solution)/shard_map/stack | solution.py:453
  1.3 1.5 %pack_rows.1 = (f32[24,256]{1,0:T(8,128)}, f32[24,256]{1,0:T(8,128)}) custom-call(s32[3]{0:T(128)} %pad_add_fusion.flags, f32[128,256]{1,0:T(8,128)} %r.5, s32[128,256]{1,0:T(8,128)} %oc.3, f32[128,256]{1,0:T(8,128)} %dg.3, f32[128,256]{1,0:T(8,128)} %ea.3, f32[128,256]{1,0:T(8,128)} %no.3, f32[128,256]{1,0:T(8,128)} %r.5, s32[128,256]{1,0:T(8,128)} %oc.3, ...), custom_call_target="tpu_custom_call" | custom-call | tf_op jit(solution)/shard_map/pack_rows/pallas_call | solution.py:48
  2.7 2.1 %collective-permute-start = (f32[24,256]{1,0:T(8,128)}, f32[24,256]{1,0:T(8,128)S(1)}, u32[]{:S(2)}, u32[]{:S(2)}) collective-permute-start(f32[24,256]{1,0:T(8,128)} %get-tuple-element.12), channel_id=1, source_target_pairs={{0,16},{1,17},{2,18},{3,19},{4,20},{5,21},{6,22},{7,23},{8,24},{9,... | collective-permute-start | bytes 73736 | tf_op jit(solution)/shard_map/ppermute | solution.py:463
  4.9 0.7 %collective-permute-start.1 = (f32[24,256]{1,0:T(8,128)}, f32[24,256]{1,0:T(8,128)S(1)}, u32[]{:S(2)}, u32[]{:S(2)}) collective-permute-start(f32[24,256]{1,0:T(8,128)} %get-tuple-element.13.own_top), channel_id=1, source_target_pairs={{16,32},{17,33},{18,34},{19,35},{20,36},{21,37},{22,38},{23,39},{2... | collective-permute-start | bytes 73736 | tf_op jit(solution)/shard_map/ppermute | solution.py:463
  5.5 0.8 %collective-permute-done.first = f32[24,256]{1,0:T(8,128)S(1)} collective-permute-done((f32[24,256]{1,0:T(8,128)}, f32[24,256]{1,0:T(8,128)S(1)}, u32[]{:S(2)}, u32[]{:S(2)}) %collective-permute-start) | collective-permute-done | bytes 24608 | tf_op jit(solution)/shard_map/ppermute | solution.py:463
  6.3 0.0 collective-permute-done.1.second
  6.3 0.6 %copy-done.4 = f32[24,256]{1,0:T(8,128)} copy-done((f32[24,256]{1,0:T(8,128)}, f32[24,256]{1,0:T(8,128)S(1)}, u32[]{:S(2)}) %copy-start.4) | copy-done | bytes 24600
  6.9 0.6 %copy-done.5 = f32[24,256]{1,0:T(8,128)} copy-done((f32[24,256]{1,0:T(8,128)}, f32[24,256]{1,0:T(8,128)S(1)}, u32[]{:S(2)}) %copy-start.5) | copy-done | bytes 24600
  7.5 2.1 %pack_cols.1 = (f32[240,128]{1,0:T(8,128)}, f32[240,128]{1,0:T(8,128)}, f32[48,256]{1,0:T(8,128)}) custom-call(s32[3]{0:T(128)} %pad_add_fusion.flags, f32[128,256]{1,0:T(8,128)} %r.5, s32[128,256]{1,0:T(8,128)} %oc.3, f32[128,256]{1,0:T(8,128)} %dg.3, f32[128,256]{1,0:T(8,128)} %ea.3, f32[128,256]{1,0:T(8,128)} %no.3, f32[24,256]{1,0:T(8,128)} %copy-done.4, ...), custom_call_target="tpu_custom_call" | custom-call | tf_op jit(solution)/shard_map/pack_cols/pallas_call | solution.py:144
  9.6 1.9 %collective-permute-start.2 = (f32[240,128]{1,0:T(8,128)}, f32[240,128]{1,0:T(8,128)S(1)}, u32[]{:S(2)}, u32[]{:S(2)}) collective-permute-start(f32[240,128]{1,0:T(8,128)} %get-tuple-element.14), channel_id=1, source_target_pairs={{0,1},{1,0},{2,3},{3,2},{4,5},{5,4},{6,7},{7,6},{8,9},{9,8},{10,11... | collective-permute-start | bytes 368648 | tf_op jit(solution)/shard_map/ppermute | solution.py:463
  11.5 1.7 %collective-permute-start.3 = (f32[240,128]{1,0:T(8,128)}, f32[240,128]{1,0:T(8,128)S(1)}, u32[]{:S(2)}, u32[]{:S(2)}) collective-permute-start(f32[240,128]{1,0:T(8,128)} %get-tuple-element.15), channel_id=1, source_target_pairs={{0,15},{1,2},{2,1},{3,4},{4,3},{5,6},{6,5},{7,8},{8,7},{9,10},{10,... | collective-permute-start | bytes 368648 | tf_op jit(solution)/shard_map/ppermute | solution.py:463
  13.2 0.0 collective-permute-done.2.chip
  13.2 0.7 %collective-permute-start.4 = (f32[240,128]{1,0:T(8,128)S(1)}, f32[240,128]{1,0:T(8,128)S(1)}, u32[]{:S(2)}, u32[]{:S(2)}) collective-permute-start(f32[240,128]{1,0:T(8,128)S(1)} %collective-permute-done.2.chip), channel_id=1, source_target_pairs={{112,127},{113,114},{114,113},{115,116},{116,115},{117,118},{118,1... | collective-permute-start | bytes 368648 | tf_op jit(solution)/shard_map/ppermute | solution.py:463
  13.9 2.1 %collective-permute-done.3.far = f32[240,128]{1,0:T(8,128)S(1)} collective-permute-done((f32[240,128]{1,0:T(8,128)}, f32[240,128]{1,0:T(8,128)S(1)}, u32[]{:S(2)}, u32[]{:S(2)}) %collective-permute-start.3) | collective-permute-done | bytes 122912 | tf_op jit(solution)/shard_map/ppermute | solution.py:463
  16.0 0.7 %collective-permute-start.5 = (f32[240,128]{1,0:T(8,128)S(1)}, f32[240,128]{1,0:T(8,128)S(1)}, u32[]{:S(2)}, u32[]{:S(2)}) collective-permute-start(f32[240,128]{1,0:T(8,128)S(1)} %collective-permute-done.3.far), channel_id=1, source_target_pairs={{112,113},{113,112},{114,115},{115,114},{116,117},{117,116},{118,1... | collective-permute-start | bytes 368648 | tf_op jit(solution)/shard_map/ppermute | solution.py:463
  16.7 0.0 collective-permute-done.4.far2
  16.7 0.0 copy-start.2
  16.7 0.0 collective-permute-done.5.chip2
  16.7 0.0 copy-start.3
  16.8 0.6 %copy-done.2 = f32[240,128]{1,0:T(8,128)} copy-done((f32[240,128]{1,0:T(8,128)}, f32[240,128]{1,0:T(8,128)S(1)}, u32[]{:S(2)}) %copy-start.2) | copy-done | bytes 122904
  17.4 0.0 copy-done.3
  17.4 3.2 %basis.1 = (f32[128,256]{1,0:T(8,128)}, f32[128,256]{1,0:T(8,128)}, f32[128,256]{1,0:T(8,128)}, f32[128,256]{1,0:T(8,128)}, f32[128,128]{1,0:T(8,128)}) custom-call(s32[3]{0:T(128)} %pad_add_fusion.flags, f32[128,256]{1,0:T(8,128)} %r.5, s32[128,256]{1,0:T(8,128)} %oc.3, f32[128,256]{1,0:T(8,128)} %dg.3, f32[128,256]{1,0:T(8,128)} %ea.3, f32[128,256]{1,0:T(8,128)} %no.3, ...), custom_call_target="tpu_custom_call" | custom-call | tf_op jit(solution)/shard_map/basis/pallas_call | solution.py:350
  20.6 29.2 %all_to_all.11 = f32[128,1,128]{2,1,0:T(1,128)} all-to-all(f32[128,1,128]{2,1,0:T(1,128)} %bitcast.9), channel_id=1, replica_groups=mesh['lat_0'=2,'lat_1'=4,'lon_0'=2,'lon_1'=4,'lon_2'=2] {'lat_0','lat_1'..., dimensions={0} | all-to-all | bytes 131072 | tf_op jit(solution)/shard_map/all_to_all | solution.py:488
  49.8 2.2 %combine.1 = (f32[128,256]{1,0:T(8,128)}, f32[128,256]{1,0:T(8,128)}) custom-call(f32[128,128]{1,0:T(8,128)} %bitcast.8, f32[128,256]{1,0:T(8,128)} %r.5, f32[128,256]{1,0:T(8,128)} %get-tuple-element.18.t1, f32[128,256]{1,0:T(8,128)} %get-tuple-element.19.t2, f32[128,256]{1,0:T(8,128)} %get-tuple-element.20.t3, f32[128,256]{1,0:T(8,128)} %get-tuple-element.21.t4), custom_call_target="tpu_custom_call" | custom-call | tf_op jit(solution)/shard_map/combine/pallas_call | solution.py:443
  (6 shorter events, 0.0 us)
Async XLA Ops:
  2.7 3.5 %collective-permute-start = (f32[24,256]{1,0:T(8,128)}, f32[24,256]{1,0:T(8,128)S(1)}, u32[]{:S(2)}, u32[]{:S(2)}) collective-permute-start(f32[24,256]{1,0:T(8,128)} %get-tuple-element.12), channel_id=1, source_target_pairs={{0,16},{1,17},{2,18},{3,19},{4,20},{5,21},{6,22},{7,23},{8,24},{9,... | collective-permute-start | bytes 73736 | tf_op jit(solution)/shard_map/ppermute | solution.py:463
  4.9 1.4 %collective-permute-start.1 = (f32[24,256]{1,0:T(8,128)}, f32[24,256]{1,0:T(8,128)S(1)}, u32[]{:S(2)}, u32[]{:S(2)}) collective-permute-start(f32[24,256]{1,0:T(8,128)} %get-tuple-element.13.own_top), channel_id=1, source_target_pairs={{16,32},{17,33},{18,34},{19,35},{20,36},{21,37},{22,38},{23,39},{2... | collective-permute-start | bytes 73736 | tf_op jit(solution)/shard_map/ppermute | solution.py:463
  6.3 0.6 %copy-start.4 = (f32[24,256]{1,0:T(8,128)}, f32[24,256]{1,0:T(8,128)S(1)}, u32[]{:S(2)}) copy-start(f32[24,256]{1,0:T(8,128)S(1)} %collective-permute-done.first) | copy-start | bytes 73732
  6.9 0.6 %copy-start.5 = (f32[24,256]{1,0:T(8,128)}, f32[24,256]{1,0:T(8,128)S(1)}, u32[]{:S(2)}) copy-start(f32[24,256]{1,0:T(8,128)S(1)} %collective-permute-done.1.second) | copy-start | bytes 73732
  9.6 3.6 %collective-permute-start.2 = (f32[240,128]{1,0:T(8,128)}, f32[240,128]{1,0:T(8,128)S(1)}, u32[]{:S(2)}, u32[]{:S(2)}) collective-permute-start(f32[240,128]{1,0:T(8,128)} %get-tuple-element.14), channel_id=1, source_target_pairs={{0,1},{1,0},{2,3},{3,2},{4,5},{5,4},{6,7},{7,6},{8,9},{9,8},{10,11... | collective-permute-start | bytes 368648 | tf_op jit(solution)/shard_map/ppermute | solution.py:463
  11.5 4.5 %collective-permute-start.3 = (f32[240,128]{1,0:T(8,128)}, f32[240,128]{1,0:T(8,128)S(1)}, u32[]{:S(2)}, u32[]{:S(2)}) collective-permute-start(f32[240,128]{1,0:T(8,128)} %get-tuple-element.15), channel_id=1, source_target_pairs={{0,15},{1,2},{2,1},{3,4},{4,3},{5,6},{6,5},{7,8},{8,7},{9,10},{10,... | collective-permute-start | bytes 368648 | tf_op jit(solution)/shard_map/ppermute | solution.py:463
  13.2 3.5 %copy-start = (f32[240,128]{1,0:T(8,128)}, f32[240,128]{1,0:T(8,128)S(1)}, u32[]{:S(2)}) copy-start(f32[240,128]{1,0:T(8,128)S(1)} %collective-permute-done.2.chip) | copy-start | bytes 368644
  13.2 3.5 %collective-permute-start.4 = (f32[240,128]{1,0:T(8,128)S(1)}, f32[240,128]{1,0:T(8,128)S(1)}, u32[]{:S(2)}, u32[]{:S(2)}) collective-permute-start(f32[240,128]{1,0:T(8,128)S(1)} %collective-permute-done.2.chip), channel_id=1, source_target_pairs={{112,127},{113,114},{114,113},{115,116},{116,115},{117,118},{118,1... | collective-permute-start | bytes 368648 | tf_op jit(solution)/shard_map/ppermute | solution.py:463
  16.0 0.7 %copy-start.1 = (f32[240,128]{1,0:T(8,128)}, f32[240,128]{1,0:T(8,128)S(1)}, u32[]{:S(2)}) copy-start(f32[240,128]{1,0:T(8,128)S(1)} %collective-permute-done.3.far) | copy-start | bytes 368644
  16.0 0.7 %collective-permute-start.5 = (f32[240,128]{1,0:T(8,128)S(1)}, f32[240,128]{1,0:T(8,128)S(1)}, u32[]{:S(2)}, u32[]{:S(2)}) collective-permute-start(f32[240,128]{1,0:T(8,128)S(1)} %collective-permute-done.3.far), channel_id=1, source_target_pairs={{112,113},{113,112},{114,115},{115,114},{116,117},{117,116},{118,1... | collective-permute-start | bytes 368648 | tf_op jit(solution)/shard_map/ppermute | solution.py:463
  16.7 0.7 %copy-start.2 = (f32[240,128]{1,0:T(8,128)}, f32[240,128]{1,0:T(8,128)S(1)}, u32[]{:S(2)}) copy-start(f32[240,128]{1,0:T(8,128)S(1)} %collective-permute-done.4.far2) | copy-start | bytes 368644
  16.7 0.7 %copy-start.3 = (f32[240,128]{1,0:T(8,128)}, f32[240,128]{1,0:T(8,128)S(1)}, u32[]{:S(2)}) copy-start(f32[240,128]{1,0:T(8,128)S(1)} %collective-permute-done.5.chip2) | copy-start | bytes 368644

commit v3 on v2

--- a/solution.py
+++ b/solution.py
@@ -17,6 +17,7 @@
 F32 = jnp.float32
 W = 4
 LANES = 128
+GRANT = 16 << 20
 STRIP = 48
 
 
@@ -28,34 +29,49 @@
     return jnp.concatenate(parts, axis=axis)
 
 
-def _pack_rows(flags, *refs):
-    bottoms, tops, (partner, first, second) = (refs[:5], refs[5:10], refs[10:])
-    even = flags[1] == 0
+def _pack_rows(*refs):
+    fields, partner = (refs[:5], refs[5])
+    first, second, floats, ints, order, done = refs[6:]
+    rows = fields[0].shape[0]
+    even = lax.axis_index(LAT) % 2 == 0
+    copies = []
+    for f, x in enumerate(fields):
+        for h, start in enumerate((0, rows - 8)):
+            target = ints.at[h] if f == 1 else floats.at[f, h]
+            copies.append(pltpu.make_async_copy(x.at[pl.ds(start, 8), :], target, done.at[2 * f + h]))
+    copies.append(pltpu.make_async_copy(partner, order, done.at[10]))
+    for copy in copies:
+        copy.start()
+    for copy in copies:
+        copy.wait()
     for f in range(5):
-        low = bottoms[f][0:W, :].astype(F32)
-        high = tops[f][8 - W : 8, :].astype(F32)
+        x = ints if f == 1 else floats.at[f]
+        low = x[0, 0:W, :].astype(F32)
+        high = x[1, 8 - W : 8, :].astype(F32)
         first[W * f : W * f + W, :] = jnp.where(even, high, low)
         second[W * f : W * f + W, :] = jnp.where(even, low, high)
     first[20:24, :] = jnp.zeros((4, first.shape[1]), F32)
-    second[20:24, :] = jnp.broadcast_to(partner[...].astype(F32), (4, first.shape[1]))
-
-
-def pack_rows(flags, fields, partner):
-    rows, cols = fields[0].shape
-    low = pl.BlockSpec((8, cols), lambda i: (0, 0))
-    high = pl.BlockSpec((8, cols), lambda i: (rows // 8 - 1, 0))
+    second[20:24, :] = jnp.broadcast_to(order[...].astype(F32), (4, first.shape[1]))
+
+
+def pack_rows(fields, partner):
+    cols = fields[0].shape[1]
     out = jax.ShapeDtypeStruct((24, cols), F32)
+    vmem = pl.BlockSpec(memory_space=pltpu.VMEM)
     return pl.pallas_call(
         _pack_rows,
-        grid=(1,),
-        in_specs=[pl.BlockSpec(memory_space=pltpu.SMEM)]
-        + [low] * 5
-        + [high] * 5
-        + [pl.BlockSpec((1, cols), lambda i: (0, 0))],
-        out_specs=(pl.BlockSpec((24, cols), lambda i: (0, 0)),) * 2,
+        in_specs=[pl.BlockSpec(memory_space=pltpu.HBM)] * 6,
+        out_specs=(vmem,) * 2,
         out_shape=(out, out),
+        scratch_shapes=[
+            pltpu.VMEM((5, 2, 8, cols), F32),
+            pltpu.VMEM((2, 8, cols), jnp.int32),
+            pltpu.VMEM((1, cols), jnp.int32),
+            pltpu.SemaphoreType.DMA((11,)),
+        ],
+        compiler_params=pltpu.CompilerParams(vmem_limit_bytes=GRANT),
         name="pack_rows",
-    )(flags, *fields, *fields, partner)
+    )(*fields, partner)
 
 
 def _pick(source, index):
@@ -69,12 +85,12 @@
     return _cat(outs, 1)
 
 
-def _pack_cols(flags, r, oc, dg, ea, no, first, second, own_top, to_chip, to_far, strip):
+def _pack_cols(r, oc, dg, ea, no, first, second, own_top, to_chip, to_far, strip):
     rows = r.shape[0]
     lane = _iota((1, LANES), 1)
-    on_top = flags[0] == 1
-    row_even = flags[1] == 0
-    col_even = flags[2] == 0
+    on_top = lax.axis_index(LAT) == lax.axis_size(LAT) - 1
+    row_even = lax.axis_index(LAT) % 2 == 0
+    col_even = lax.axis_index(LON) % 2 == 0
 
     def store(at, count, west, east):
         to_chip[at : at + count, :] = jnp.where(col_even, east, west)
@@ -137,17 +153,18 @@
         to_far[base + STRIP * half : base + STRIP * (half + 1), :] = part
 
 
-def pack_cols(flags, fields, first, second, own_top):
+def pack_cols(fields, first, second, own_top):
     rows, cols = fields[0].shape
     message = jax.ShapeDtypeStruct((rows + 16 + 2 * STRIP, LANES), F32)
     vmem = pl.BlockSpec(memory_space=pltpu.VMEM)
     return pl.pallas_call(
         _pack_cols,
-        in_specs=[pl.BlockSpec(memory_space=pltpu.SMEM)] + [vmem] * 8,
+        in_specs=[vmem] * 8,
         out_specs=(vmem,) * 3,
         out_shape=(message, message, jax.ShapeDtypeStruct((STRIP, cols), F32)),
+        compiler_params=pltpu.CompilerParams(vmem_limit_bytes=GRANT),
         name="pack_cols",
-    )(flags, *fields, first, second, own_top)
+    )(*fields, first, second, own_top)
 
 
 def _lanes_left(x):
@@ -232,16 +249,16 @@
         neighbour = _cat([*picked, jnp.zeros((8, LANES), F32)], 1)
 
 
-def _basis(flags, r, oc, dg, ea, no, first, second, chip, far, far2, chip2, strip, t1, t2, t3, t4, moments, ext, coef, fold, sides):
+def _basis(r, oc, dg, ea, no, first, second, chip, far, far2, chip2, strip, t1, t2, t3, t4, moments, ext, coef, fold, sides):
     rows, cols = r.shape
     pad = 16
     high = rows + pad
     wide = cols + LANES
     lane = _iota((1, LANES), 1)
     total = rows + 2 * pad
-    on_top = flags[0] == 1
-    row_even = flags[1] == 0
-    col_even = flags[2] == 0
+    on_top = lax.axis_index(LAT) == lax.axis_size(LAT) - 1
+    row_even = lax.axis_index(LAT) % 2 == 0
+    col_even = lax.axis_index(LON) % 2 == 0
     for f, own in enumerate((r, oc, dg, ea, no)):
         ext[f, 0 : pad, :cols] = jnp.zeros((pad, cols), F32)
         ext[f, high : high + pad, :cols] = jnp.zeros((pad, cols), F32)
@@ -343,13 +360,13 @@
     moments[...] = jnp.broadcast_to(out, moments.shape)
 
 
-def basis(flags, fields, first, second, chip, far, far2, chip2, strip, devices):
+def basis(fields, first, second, chip, far, far2, chip2, strip, devices):
     rows, cols = fields[0].shape
     vmem = pl.BlockSpec(memory_space=pltpu.VMEM)
     out = jax.ShapeDtypeStruct((rows, cols), F32)
     return pl.pallas_call(
         _basis,
-        in_specs=[pl.BlockSpec(memory_space=pltpu.SMEM)] + [vmem] * 12,
+        in_specs=[vmem] * 12,
         out_specs=(vmem,) * 5,
         out_shape=(out,) * 4 + (jax.ShapeDtypeStruct((devices, LANES), F32),),
         scratch_shapes=[
@@ -358,8 +375,9 @@
             pltpu.VMEM((8, cols + LANES), F32),
             pltpu.VMEM((4, 2 * STRIP, LANES), F32),
         ],
+        compiler_params=pltpu.CompilerParams(vmem_limit_bytes=GRANT),
         name="basis",
-    )(flags, *fields, first, second, chip, far, far2, chip2, strip)
+    )(*fields, first, second, chip, far, far2, chip2, strip)
 
 
 def _combine(gathered, r, t1, t2, t3, t4, x_out, r_out):
@@ -441,7 +459,12 @@
     vmem = pl.BlockSpec(memory_space=pltpu.VMEM)
     out = jax.ShapeDtypeStruct(r.shape, F32)
     return pl.pallas_call(
-        _combine, in_specs=[vmem] * 6, out_specs=(vmem,) * 2, out_shape=(out, out), name="combine"
+        _combine,
+        in_specs=[vmem] * 6,
+        out_specs=(vmem,) * 2,
+        out_shape=(out, out),
+        compiler_params=pltpu.CompilerParams(vmem_limit_bytes=GRANT),
+        name="combine",
     )(gathered, r, t1, t2, t3, t4)
 
 
@@ -449,8 +472,6 @@
     cols = right_side.shape[1]
     lats, lons = (lax.axis_size(LAT), lax.axis_size(LON))
     devices = lats * lons
-    lat, lon = (lax.axis_index(LAT), lax.axis_index(LON))
-    flags = jnp.stack([(lat == lats - 1).astype(jnp.int32), lat % 2, lon % 2])
     fields = (right_side, land_sea, diagonal, east_coef, north_coef)
 
     def swap(x, partner, rows=range(lats)):
@@ -476,15 +497,16 @@
         return (i, j ^ 1)
 
     top = (lats - 1,)
-    to_first, to_second = pack_rows(flags, fields, fold_partner.reshape(1, cols))
+    kept = [pltpu.with_memory_space_constraint(x, pltpu.HBM) for x in (*fields, fold_partner.reshape(1, cols))]
+    to_first, to_second = pack_rows(kept[:5], kept[5])
     first = swap(to_first, lambda i, j: (i ^ 1, j))
     second = swap(to_second, second_row)
-    to_chip, to_far, strip = pack_cols(flags, fields, first, second, to_second)
+    to_chip, to_far, strip = pack_cols(fields, first, second, to_second)
     chip = swap(to_chip, on_chip)
     far = swap(to_far, off_chip)
     far2 = swap(chip, off_chip, top)
     chip2 = swap(far, on_chip, top)
-    t1, t2, t3, t4, moments = basis(flags, fields, first, second, chip, far, far2, chip2, strip, devices)
+    t1, t2, t3, t4, moments = basis(fields, first, second, chip, far, far2, chip2, strip, devices)
     gathered = lax.all_to_all(moments, LAT_LON, 0, 0)
     return combine(gathered, right_side, t1, t2, t3, t4)
 

time: 52.4 us -> 43.9 us (0.84)
  Pallas kernels: 9.03 us -> 3.52 us
  local copies, waits for them, and re-layouts: 1.86 us -> 0.02 us
  other arithmetic: 0.62 us -> 0 us
    pallas_call x3, Pallas kernels: 6.78 us -> 2.44 us  [the longest x1 1.21 us: basis(): pl.pallas_call(_basis, in_specs=[vmem] * 12, out_specs=(vmem,) * 5, out_s...]
    unnamed x12 -> x10, local copies, waits for them, and re-layouts: 1.86 us -> 0.02 us
    pallas_call x1, Pallas kernels: 2.24 us -> 1.08 us  [combine(): pl.pallas_call(_combine, in_specs=[vmem] * 6, out_specs=(vmem,) * 2, out_...]
    another operation x1 -> x0, other arithmetic: 0.62 us -> none  [local(): flags = jnp.stack([(lat == lats - 1).astype(jnp.int32), lat % 2, lon % 2])]
where the time goes in v3:
time: 43.9 us; the launch traced here: 43.7 us
  blocking collectives  29.1 us (66%)
  starting transfers between devices  7.84 us (18%)
  Pallas kernels  3.52 us (8%)
  waiting for transfers between devices  2.48 us (6%)
  between operations  0.76 us (2%)
    all_to_all x1, blocking collectives, local(): gathered = lax.all_to_all(moments, LAT_LON, 0, 0)  29.1 us
    ppermute x6, starting transfers between devices, swap(): return lax.ppermute(x, LAT_LON, pairs)  7.84 us
    ppermute x6, waiting for transfers between devices, swap(): return lax.ppermute(x, LAT_LON, pairs)  2.48 us
    pallas_call x1, Pallas kernels, basis(): pl.pallas_call(_basis, in_specs=[vmem] * 12, out_specs=(vmem,) * 5, out_s...  1.21 us
    pallas_call x1, Pallas kernels, combine(): pl.pallas_call(_combine, in_specs=[vmem] * 6, out_specs=(vmem,) * 2, out_...  1.08 us
    pallas_call x1, Pallas kernels, pack_rows(): pl.pallas_call(_pack_rows, in_specs=[pl.BlockSpec(memory_space=pltpu.HBM)...  0.99 us
  transfers between devices with their start and end apart: 6, of which 2 were waited for; matrix products, arithmetic and copies ran while one was open for 0% of the time, Pallas kernels for 0%

profile of v3, /device:TPU:1, one launch (start us, length us, event | category | flops | bytes accessed | tf_op | source)
XLA Modules:
  0.0 43.7 jit_solution(3153141606097902780)
XLA Ops:
  0.6 0.0 copy-start
  0.6 0.0 copy-start.1
  0.7 0.0 copy-start.2
  0.7 0.0 copy-start.3
  0.7 0.0 copy-start.4
  0.7 1.0 %pack_rows.1 = (f32[24,256]{1,0:T(8,128)S(1)}, f32[24,256]{1,0:T(8,128)S(1)}) custom-call(f32[128,256]{1,0:T(8,128)} %r.5, s32[128,256]{1,0:T(8,128)} %oc.3, f32[128,256]{1,0:T(8,128)} %dg.3, f32[128,256]{1,0:T(8,128)} %ea.3, f32[128,256]{1,0:T(8,128)} %no.3, s32[1,256]{1,0:T(1,128)} %bitcast.7), custom_call_target="tpu_custom_call" | custom-call | tf_op jit(solution)/shard_map/pack_rows/pallas_call | solution.py:61
  1.7 2.2 %collective-permute-start = (f32[24,256]{1,0:T(8,128)S(1)}, f32[24,256]{1,0:T(8,128)S(1)}, u32[]{:S(2)}, u32[]{:S(2)}) collective-permute-start(f32[24,256]{1,0:T(8,128)S(1)} %get-tuple-element.12), channel_id=1, source_target_pairs={{0,16},{1,17},{2,18},{3,19},{4,20},{5,21},{6,22},{7,23},{8,24},{9,... | collective-permute-start | bytes 73736 | tf_op jit(solution)/shard_map/ppermute | solution.py:484
  3.9 0.7 %collective-permute-start.1 = (f32[24,256]{1,0:T(8,128)S(1)}, f32[24,256]{1,0:T(8,128)S(1)}, u32[]{:S(2)}, u32[]{:S(2)}) collective-permute-start(f32[24,256]{1,0:T(8,128)S(1)} %get-tuple-element.13.own_top), channel_id=1, source_target_pairs={{16,32},{17,33},{18,34},{19,35},{20,36},{21,37},{22,38},{23,39},{2... | collective-permute-start | bytes 73736 | tf_op jit(solution)/shard_map/ppermute | solution.py:484
  4.5 0.6 %collective-permute-done.first = f32[24,256]{1,0:T(8,128)S(1)} collective-permute-done((f32[24,256]{1,0:T(8,128)S(1)}, f32[24,256]{1,0:T(8,128)S(1)}, u32[]{:S(2)}, u32[]{:S(2)}) %collective-permute-start) | collective-permute-done | bytes 24608 | tf_op jit(solution)/shard_map/ppermute | solution.py:484
  5.1 0.0 collective-permute-done.1.second
  5.1 0.0 copy-done
  5.1 0.0 copy-done.1
  5.1 0.2 pack_cols.1
  5.4 2.0 %collective-permute-start.2 = (f32[240,128]{1,0:T(8,128)S(1)}, f32[240,128]{1,0:T(8,128)S(1)}, u32[]{:S(2)}, u32[]{:S(2)}) collective-permute-start(f32[240,128]{1,0:T(8,128)S(1)} %get-tuple-element.14), channel_id=1, source_target_pairs={{0,1},{1,0},{2,3},{3,2},{4,5},{5,4},{6,7},{7,6},{8,9},{9,8},{10,11... | collective-permute-start | bytes 368648 | tf_op jit(solution)/shard_map/ppermute | solution.py:484
  7.3 1.7 %collective-permute-start.3 = (f32[240,128]{1,0:T(8,128)S(1)}, f32[240,128]{1,0:T(8,128)S(1)}, u32[]{:S(2)}, u32[]{:S(2)}) collective-permute-start(f32[240,128]{1,0:T(8,128)S(1)} %get-tuple-element.15), channel_id=1, source_target_pairs={{0,15},{1,2},{2,1},{3,4},{4,3},{5,6},{6,5},{7,8},{8,7},{9,10},{10,... | collective-permute-start | bytes 368648 | tf_op jit(solution)/shard_map/ppermute | solution.py:484
  9.1 0.0 collective-permute-done.2.chip
  9.1 0.7 %collective-permute-start.4 = (f32[240,128]{1,0:T(8,128)S(1)}, f32[240,128]{1,0:T(8,128)S(1)}, u32[]{:S(2)}, u32[]{:S(2)}) collective-permute-start(f32[240,128]{1,0:T(8,128)S(1)} %collective-permute-done.2.chip), channel_id=1, source_target_pairs={{112,127},{113,114},{114,113},{115,116},{116,115},{117,118},{118,1... | collective-permute-start | bytes 368648 | tf_op jit(solution)/shard_map/ppermute | solution.py:484
  9.7 1.9 %collective-permute-done.3.far = f32[240,128]{1,0:T(8,128)S(1)} collective-permute-done((f32[240,128]{1,0:T(8,128)S(1)}, f32[240,128]{1,0:T(8,128)S(1)}, u32[]{:S(2)}, u32[]{:S(2)}) %collective-permute-start.3) | collective-permute-done | bytes 122912 | tf_op jit(solution)/shard_map/ppermute | solution.py:484
  11.6 0.7 %collective-permute-start.5 = (f32[240,128]{1,0:T(8,128)S(1)}, f32[240,128]{1,0:T(8,128)S(1)}, u32[]{:S(2)}, u32[]{:S(2)}) collective-permute-start(f32[240,128]{1,0:T(8,128)S(1)} %collective-permute-done.3.far), channel_id=1, source_target_pairs={{112,113},{113,112},{114,115},{115,114},{116,117},{117,116},{118,1... | collective-permute-start | bytes 368648 | tf_op jit(solution)/shard_map/ppermute | solution.py:484
  12.3 0.0 collective-permute-done.4.far2
  12.3 0.0 collective-permute-done.5.chip2
  12.3 1.2 %basis.1 = (f32[128,256]{1,0:T(8,128)S(1)}, f32[128,256]{1,0:T(8,128)S(1)}, f32[128,256]{1,0:T(8,128)S(1)}, f32[128,256]{1,0:T(8,128)S(1)}, f32[128,128]{1,0:T(8,128)S(1)}) custom-call(f32[128,256]{1,0:T(8,128)S(1)} %copy-done, s32[128,256]{1,0:T(8,128)S(1)} %copy-done.1, f32[128,256]{1,0:T(8,128)S(1)} %copy-done.2, f32[128,256]{1,0:T(8,128)S(1)} %copy-done.3, ...), custom_call_target="tpu_custom_call" | custom-call | tf_op jit(solution)/shard_map/basis/pallas_call | solution.py:367
  13.5 29.1 %all_to_all.11 = f32[128,1,128]{2,1,0:T(1,128)S(1)} all-to-all(f32[128,1,128]{2,1,0:T(1,128)S(1)} %bitcast.6), channel_id=1, replica_groups=mesh['lat_0'=2,'lat_1'=4,'lon_0'=2,'lon_1'=4,'lon_2'=2] {'lat_0','lat_1'..., dimensions={0} | all-to-all | bytes 131072 | tf_op jit(solution)/shard_map/all_to_all | solution.py:510
  42.7 1.1 %combine.1 = (f32[128,256]{1,0:T(8,128)}, f32[128,256]{1,0:T(8,128)}) custom-call(f32[128,128]{1,0:T(8,128)S(1)} %bitcast.5, f32[128,256]{1,0:T(8,128)S(1)} %copy-done, f32[128,256]{1,0:T(8,128)S(1)} %get-tuple-element.18.t1, f32[128,256]{1,0:T(8,128)S(1)} %get-tuple-element.19.t2, f32[128,256]{1,0:T(8,128)S(1)} %get-tuple-element.20.t3, ...), custom_call_target="tpu_custom_call" | custom-call | tf_op jit(solution)/shard_map/combine/pallas_call | solution.py:461
  (3 shorter events, 0.0 us)
Async XLA Ops:
  0.6 4.5 %copy-start = (f32[128,256]{1,0:T(8,128)S(1)}, f32[128,256]{1,0:T(8,128)}, u32[]{:S(2)}) copy-start(f32[128,256]{1,0:T(8,128)} %r.5) | copy-start | bytes 393220
  0.6 4.5 %copy-start.1 = (s32[128,256]{1,0:T(8,128)S(1)}, s32[128,256]{1,0:T(8,128)}, u32[]{:S(2)}) copy-start(s32[128,256]{1,0:T(8,128)} %oc.3) | copy-start | bytes 393220
  0.7 4.4 %copy-start.2 = (f32[128,256]{1,0:T(8,128)S(1)}, f32[128,256]{1,0:T(8,128)}, u32[]{:S(2)}) copy-start(f32[128,256]{1,0:T(8,128)} %dg.3) | copy-start | bytes 393220
  0.7 4.4 %copy-start.3 = (f32[128,256]{1,0:T(8,128)S(1)}, f32[128,256]{1,0:T(8,128)}, u32[]{:S(2)}) copy-start(f32[128,256]{1,0:T(8,128)} %ea.3) | copy-start | bytes 393220
  0.7 4.4 %copy-start.4 = (f32[128,256]{1,0:T(8,128)S(1)}, f32[128,256]{1,0:T(8,128)}, u32[]{:S(2)}) copy-start(f32[128,256]{1,0:T(8,128)} %no.3) | copy-start | bytes 393220
  1.7 3.4 %collective-permute-start = (f32[24,256]{1,0:T(8,128)S(1)}, f32[24,256]{1,0:T(8,128)S(1)}, u32[]{:S(2)}, u32[]{:S(2)}) collective-permute-start(f32[24,256]{1,0:T(8,128)S(1)} %get-tuple-element.12), channel_id=1, source_target_pairs={{0,16},{1,17},{2,18},{3,19},{4,20},{5,21},{6,22},{7,23},{8,24},{9,... | collective-permute-start | bytes 73736 | tf_op jit(solution)/shard_map/ppermute | solution.py:484
  3.9 1.2 %collective-permute-start.1 = (f32[24,256]{1,0:T(8,128)S(1)}, f32[24,256]{1,0:T(8,128)S(1)}, u32[]{:S(2)}, u32[]{:S(2)}) collective-permute-start(f32[24,256]{1,0:T(8,128)S(1)} %get-tuple-element.13.own_top), channel_id=1, source_target_pairs={{16,32},{17,33},{18,34},{19,35},{20,36},{21,37},{22,38},{23,39},{2... | collective-permute-start | bytes 73736 | tf_op jit(solution)/shard_map/ppermute | solution.py:484
  5.4 3.7 %collective-permute-start.2 = (f32[240,128]{1,0:T(8,128)S(1)}, f32[240,128]{1,0:T(8,128)S(1)}, u32[]{:S(2)}, u32[]{:S(2)}) collective-permute-start(f32[240,128]{1,0:T(8,128)S(1)} %get-tuple-element.14), channel_id=1, source_target_pairs={{0,1},{1,0},{2,3},{3,2},{4,5},{5,4},{6,7},{7,6},{8,9},{9,8},{10,11... | collective-permute-start | bytes 368648 | tf_op jit(solution)/shard_map/ppermute | solution.py:484
  7.3 4.3 %collective-permute-start.3 = (f32[240,128]{1,0:T(8,128)S(1)}, f32[240,128]{1,0:T(8,128)S(1)}, u32[]{:S(2)}, u32[]{:S(2)}) collective-permute-start(f32[240,128]{1,0:T(8,128)S(1)} %get-tuple-element.15), channel_id=1, source_target_pairs={{0,15},{1,2},{2,1},{3,4},{4,3},{5,6},{6,5},{7,8},{8,7},{9,10},{10,... | collective-permute-start | bytes 368648 | tf_op jit(solution)/shard_map/ppermute | solution.py:484
  9.1 3.2 %collective-permute-start.4 = (f32[240,128]{1,0:T(8,128)S(1)}, f32[240,128]{1,0:T(8,128)S(1)}, u32[]{:S(2)}, u32[]{:S(2)}) collective-permute-start(f32[240,128]{1,0:T(8,128)S(1)} %collective-permute-done.2.chip), channel_id=1, source_target_pairs={{112,127},{113,114},{114,113},{115,116},{116,115},{117,118},{118,1... | collective-permute-start | bytes 368648 | tf_op jit(solution)/shard_map/ppermute | solution.py:484
  11.6 0.7 %collective-permute-start.5 = (f32[240,128]{1,0:T(8,128)S(1)}, f32[240,128]{1,0:T(8,128)S(1)}, u32[]{:S(2)}, u32[]{:S(2)}) collective-permute-start(f32[240,128]{1,0:T(8,128)S(1)} %collective-permute-done.3.far), channel_id=1, source_target_pairs={{112,113},{113,112},{114,115},{115,114},{116,117},{117,116},{118,1... | collective-permute-start | bytes 368648 | tf_op jit(solution)/shard_map/ppermute | solution.py:484

commit v4 on v3

--- a/solution.py
+++ b/solution.py
@@ -31,9 +31,8 @@
 
 def _pack_rows(*refs):
     fields, partner = (refs[:5], refs[5])
-    first, second, floats, ints, order, done = refs[6:]
+    record, floats, ints, order, done = refs[6:]
     rows = fields[0].shape[0]
-    even = lax.axis_index(LAT) % 2 == 0
     copies = []
     for f, x in enumerate(fields):
         for h, start in enumerate((0, rows - 8)):
@@ -46,23 +45,19 @@
         copy.wait()
     for f in range(5):
         x = ints if f == 1 else floats.at[f]
-        low = x[0, 0:W, :].astype(F32)
-        high = x[1, 8 - W : 8, :].astype(F32)
-        first[W * f : W * f + W, :] = jnp.where(even, high, low)
-        second[W * f : W * f + W, :] = jnp.where(even, low, high)
-    first[20:24, :] = jnp.zeros((4, first.shape[1]), F32)
-    second[20:24, :] = jnp.broadcast_to(order[...].astype(F32), (4, first.shape[1]))
+        record[W * f : W * f + W, :] = x[0, 0:W, :].astype(F32)
+        record[24 + W * f : 24 + W * f + W, :] = x[1, 8 - W : 8, :].astype(F32)
+    record[20:24, :] = jnp.zeros((4, record.shape[1]), F32)
+    record[44:48, :] = jnp.broadcast_to(order[...].astype(F32), (4, record.shape[1]))
 
 
 def pack_rows(fields, partner):
     cols = fields[0].shape[1]
-    out = jax.ShapeDtypeStruct((24, cols), F32)
-    vmem = pl.BlockSpec(memory_space=pltpu.VMEM)
     return pl.pallas_call(
         _pack_rows,
         in_specs=[pl.BlockSpec(memory_space=pltpu.HBM)] * 6,
-        out_specs=(vmem,) * 2,
-        out_shape=(out, out),
+        out_specs=pl.BlockSpec(memory_space=pltpu.VMEM),
+        out_shape=jax.ShapeDtypeStruct((48, cols), F32),
         scratch_shapes=[
             pltpu.VMEM((5, 2, 8, cols), F32),
             pltpu.VMEM((2, 8, cols), jnp.int32),
@@ -74,6 +69,32 @@
     )(*fields, partner)
 
 
+def _places():
+    lat, core = (lax.axis_index(LAT), lax.axis_index(LON) % 2)
+    return (lat == lax.axis_size(LAT) - 1, core == 0, (lat + core) % 2 == 0)
+
+
+def _pack_chip(mine, sibling, out):
+    _, western, northern = _places()
+    for slot in range(2):
+        first, second = (mine, sibling) if slot == 0 else (sibling, mine)
+        low = jnp.where(western, first[0:24, :], second[0:24, :])
+        high = jnp.where(western, first[24:48, :], second[24:48, :])
+        out[24 * slot : 24 * slot + 24, :] = jnp.where(northern, high, low)
+
+
+def pack_chip(mine, sibling):
+    vmem = pl.BlockSpec(memory_space=pltpu.VMEM)
+    return pl.pallas_call(
+        _pack_chip,
+        in_specs=[vmem] * 2,
+        out_specs=vmem,
+        out_shape=jax.ShapeDtypeStruct(mine.shape, F32),
+        compiler_params=pltpu.CompilerParams(vmem_limit_bytes=GRANT),
+        name="pack_chip",
+    )(mine, sibling)
+
+
 def _pick(source, index):
     low = index & (LANES - 1)
     outs = []
@@ -85,16 +106,24 @@
     return _cat(outs, 1)
 
 
-def _pack_cols(r, oc, dg, ea, no, first, second, own_top, to_chip, to_far, strip):
+def _edges(lane, left, right):
+    return jnp.where(lane < LANES // 2, left, right)
+
+
+def _pack_cols(r, oc, dg, ea, no, mine, sibling, traded, told, to_chip, to_far, halo, strips):
     rows = r.shape[0]
     lane = _iota((1, LANES), 1)
-    on_top = lax.axis_index(LAT) == lax.axis_size(LAT) - 1
-    row_even = lax.axis_index(LAT) % 2 == 0
-    col_even = lax.axis_index(LON) % 2 == 0
+    on_top, western, northern = _places()
+    slots = []
+    for choose in (northern, jnp.logical_not(northern)):
+        slots.append([jnp.where(choose, traded[k : k + 24, :], told[k : k + 24, :]) for k in (0, 24)])
+    north, south = slots
+    halo[0:24, :] = jnp.where(western, north[0], north[1])
+    halo[24:48, :] = jnp.where(western, south[0], south[1])
 
     def store(at, count, west, east):
-        to_chip[at : at + count, :] = jnp.where(col_even, east, west)
-        to_far[at : at + count, :] = jnp.where(col_even, west, east)
+        to_chip[at : at + count, :] = jnp.where(western, east, west)
+        to_far[at : at + count, :] = jnp.where(western, west, east)
 
     def packed(pieces):
         west = east = None
@@ -117,10 +146,10 @@
             [(x[span, :LANES].astype(F32), x[span, LANES:].astype(F32)) for x in (r, oc, dg, ea, no)]
         )
         store(8 + start, 32, west, east)
-    for base, blank, choose in ((4, 0, row_even), (8 + rows, 12 + rows, jnp.logical_not(row_even))):
+    for base, blank, source in ((4, 0, 24), (8 + rows, 12 + rows, 0)):
         pieces = []
         for f in range(5):
-            x = jnp.where(choose, second[W * f : W * f + W, :], first[W * f : W * f + W, :])
+            x = halo[source + W * f : source + W * f + W, :]
             pieces.append((x[:, :LANES], x[:, LANES:]))
         west, east = packed(pieces)
         store(base, W, west, east)
@@ -128,43 +157,56 @@
 
     @pl.when(on_top)
     def _():
-        for f in range(5):
-            strip[8 * f : 8 * f + W, :] = own_top[W * f : W * f + W, :]
-            strip[8 * f + W : 8 * f + 8, :] = second[W * f : W * f + W, :]
-        strip[40:48, :] = jnp.zeros((8, 2 * LANES), F32)
-        own_partner, far_partner = (own_top[20:21, :], second[20:21, :])
-        strip[40:41, :] = own_partner
-        strip[41:42, :] = far_partner
         row = _iota((8, 1), 0)
-        index = jnp.where(row < 4, own_partner, far_partner).astype(jnp.int32) & (2 * LANES - 1)
-        masked = strip[0:8, :] * strip[8:16, :]
-        first = _pick(pltpu.roll(masked, 4, 0), index)
-        north = strip[32:40, :]
-        coef = 0.5 * (north + _pick(pltpu.roll(north, 4, 0), index))
-        strip[35:36, :] = coef[3:4, :]
-        strip[39:40, :] = coef[7:8, :]
-        strip[42:43, :] = first[3:4, :]
-        strip[43:44, :] = first[7:8, :]
+        for s, near, far in (
+            (0, mine, jnp.where(western, north[1], north[0])),
+            (STRIP, sibling, jnp.where(western, north[0], north[1])),
+        ):
+            for f in range(5):
+                strips[s + 8 * f : s + 8 * f + W, :] = near[24 + W * f : 24 + W * f + W, :]
+                strips[s + 8 * f + W : s + 8 * f + 8, :] = far[W * f : W * f + W, :]
+            strips[s + 40 : s + 48, :] = jnp.zeros((8, 2 * LANES), F32)
+            near_partner, far_partner = (near[44:45, :], far[20:21, :])
+            strips[s + 40 : s + 41, :] = near_partner
+            strips[s + 41 : s + 42, :] = far_partner
+            index = jnp.where(row < 4, near_partner, far_partner).astype(jnp.int32) & (2 * LANES - 1)
+            masked = strips[s : s + 8, :] * strips[s + 8 : s + 16, :]
+            first = _pick(pltpu.roll(masked, 4, 0), index)
+            coef = strips[s + 32 : s + 40, :]
+            coef = 0.5 * (coef + _pick(pltpu.roll(coef, 4, 0), index))
+            strips[s + 35 : s + 36, :] = coef[3:4, :]
+            strips[s + 39 : s + 40, :] = coef[7:8, :]
+            strips[s + 42 : s + 43, :] = first[3:4, :]
+            strips[s + 43 : s + 44, :] = first[7:8, :]
 
     base = rows + 16
-    for half in range(2):
-        part = strip[:, half * LANES : (half + 1) * LANES]
-        to_chip[base + STRIP * half : base + STRIP * (half + 1), :] = part
-        to_far[base + STRIP * half : base + STRIP * (half + 1), :] = part
-
-
-def pack_cols(fields, first, second, own_top):
+    to_far[base : base + STRIP, :] = strips[0:STRIP, :LANES]
+    to_far[base + STRIP : base + 2 * STRIP, :] = strips[0:STRIP, LANES:]
+    to_far[base + 2 * STRIP : base + 3 * STRIP, :] = _edges(
+        lane, strips[STRIP : 2 * STRIP, :LANES], strips[STRIP : 2 * STRIP, LANES:]
+    )
+
+
+def pack_cols(fields, mine, sibling, traded, told):
     rows, cols = fields[0].shape
-    message = jax.ShapeDtypeStruct((rows + 16 + 2 * STRIP, LANES), F32)
+
+    def out(*shape):
+        return jax.ShapeDtypeStruct(shape, F32)
+
     vmem = pl.BlockSpec(memory_space=pltpu.VMEM)
     return pl.pallas_call(
         _pack_cols,
-        in_specs=[vmem] * 8,
-        out_specs=(vmem,) * 3,
-        out_shape=(message, message, jax.ShapeDtypeStruct((STRIP, cols), F32)),
+        in_specs=[vmem] * 9,
+        out_specs=(vmem,) * 4,
+        out_shape=(
+            out(rows + 16, LANES),
+            out(rows + 16 + 3 * STRIP, LANES),
+            out(48, cols),
+            out(2 * STRIP, cols),
+        ),
         compiler_params=pltpu.CompilerParams(vmem_limit_bytes=GRANT),
         name="pack_cols",
-    )(*fields, first, second, own_top)
+    )(*fields, mine, sibling, traded, told)
 
 
 def _lanes_left(x):
@@ -175,35 +217,28 @@
     return pltpu.roll(x, 1, 1)
 
 
-def _strip_levels(strip, sides, fold):
+def _strip_levels(strips, sides, ends, fold):
     row = _iota((8, 1), 0)
     lane = _iota((1, LANES), 1)
     near = row < 4
 
-    def far(side, at, count):
-        return _cat([sides[side, at : at + count, :], sides[side, STRIP + at : STRIP + at + count, :]], 1)
-
     def assembled(mine, east, west, east2, west2):
         left = jnp.where(near, west, east)
         right = jnp.where(near, east, west)
-        tail = jnp.where(
-            lane < 64,
-            jnp.where(near, east2, west2)[:, :LANES],
-            jnp.where(near, west2, east2)[:, LANES:],
-        )
+        tail = _edges(lane, jnp.where(near, east2, west2), jnp.where(near, west2, east2))
         return _cat([left, mine, right, tail], 1)
 
     def field(f):
-        s = 8 * f
-        return assembled(strip[s : s + 8, :], *(far(side, s, 8) for side in range(4)))
+        s = slice(8 * f, 8 * f + 8)
+        return assembled(strips[s, :], sides[0, s, :], sides[1, s, :], ends[0, s, :], ends[1, s, :])
 
     def pair(at):
-        def one(a, b):
-            return jnp.where(near, a, b)
-
+        def one(x):
+            return jnp.where(near, x[0:1, :], x[1:2, :])
+
+        s = slice(at, at + 2)
         return assembled(
-            one(strip[at : at + 1, :], strip[at + 1 : at + 2, :]),
-            *(one(far(side, at, 1), far(side, at + 1, 1)) for side in range(4)),
+            one(strips[s, :]), one(sides[0, s, :]), one(sides[1, s, :]), one(ends[0, s, :]), one(ends[1, s, :])
         )
 
     r, oc, dg, ea, no = [field(f) for f in range(5)]
@@ -249,32 +284,29 @@
         neighbour = _cat([*picked, jnp.zeros((8, LANES), F32)], 1)
 
 
-def _basis(r, oc, dg, ea, no, first, second, chip, far, far2, chip2, strip, t1, t2, t3, t4, moments, ext, coef, fold, sides):
+def _basis(r, oc, dg, ea, no, halo, chip, far, chip2, strips, t1, t2, t3, t4, moments, ext, coef, fold, sides, ends):
     rows, cols = r.shape
     pad = 16
     high = rows + pad
     wide = cols + LANES
     lane = _iota((1, LANES), 1)
     total = rows + 2 * pad
-    on_top = lax.axis_index(LAT) == lax.axis_size(LAT) - 1
-    row_even = lax.axis_index(LAT) % 2 == 0
-    col_even = lax.axis_index(LON) % 2 == 0
+    on_top, western, _ = _places()
     for f, own in enumerate((r, oc, dg, ea, no)):
         ext[f, 0 : pad, :cols] = jnp.zeros((pad, cols), F32)
         ext[f, high : high + pad, :cols] = jnp.zeros((pad, cols), F32)
         ext[f, pad:high, :cols] = own[...].astype(F32)
-        one, two = (first[W * f : W * f + W, :], second[W * f : W * f + W, :])
-        ext[f, pad - W : pad, :cols] = jnp.where(row_even, two, one)
-        ext[f, high : high + W, :cols] = jnp.where(row_even, one, two)
+        ext[f, pad - W : pad, :cols] = halo[24 + W * f : 24 + W * f + W, :]
+        ext[f, high : high + W, :cols] = halo[W * f : W * f + W, :]
         ext[f, 0:8, cols:] = jnp.zeros((8, LANES), F32)
         ext[f, total - 8 : total, cols:] = jnp.zeros((8, LANES), F32)
-        east = jnp.where(col_even, chip[0 : rows + 16, :], far[0 : rows + 16, :])
+        east = jnp.where(western, chip[0 : rows + 16, :], far[0 : rows + 16, :])
         if f:
             east = pltpu.roll(east, LANES - W * f, 1)
-        west = jnp.where(col_even, far[0 : rows + 16, :], chip[0 : rows + 16, :])
+        west = jnp.where(western, far[0 : rows + 16, :], chip[0 : rows + 16, :])
         west = pltpu.roll(west, LANES - W - W * f, 1)
-        halo = jnp.where(lane < W, east, jnp.where(lane >= LANES - W, west, 0.0))
-        ext[f, 8 : 8 + rows + 16, cols:] = halo
+        outer = jnp.where(lane < W, east, jnp.where(lane >= LANES - W, west, 0.0))
+        ext[f, 8 : 8 + rows + 16, cols:] = outer
     for k in (5, 6, 7):
         ext[k, 0:8, :] = jnp.zeros((8, wide), F32)
         ext[k, total - 8 : total, :] = jnp.zeros((8, wide), F32)
@@ -282,12 +314,16 @@
     @pl.when(on_top)
     def _():
         ext[4, high - 1 : high, :] = jnp.zeros((1, wide), F32)
-        tail = slice(rows + 16, rows + 16 + 2 * STRIP)
-        sides[0] = jnp.where(col_even, chip[tail, :], far[tail, :])
-        sides[1] = jnp.where(col_even, far[tail, :], chip[tail, :])
-        sides[2] = jnp.where(col_even, chip2[tail, :], far2[tail, :])
-        sides[3] = jnp.where(col_even, far2[tail, :], chip2[tail, :])
-        _strip_levels(strip, sides, fold)
+        base = rows + 16
+        near = strips[STRIP : 2 * STRIP, :]
+        beyond = _cat([far[base : base + STRIP, :], far[base + STRIP : base + 2 * STRIP, :]], 1)
+        sides[0] = jnp.where(western, near, beyond)
+        sides[1] = jnp.where(western, beyond, near)
+        near = _edges(lane, chip2[base : base + STRIP, :], chip2[base + STRIP : base + 2 * STRIP, :])
+        beyond = far[base + 2 * STRIP : base + 3 * STRIP, :]
+        ends[0] = jnp.where(western, near, beyond)
+        ends[1] = jnp.where(western, beyond, near)
+        _strip_levels(strips, sides, ends, fold)
 
     @pl.when(jnp.logical_not(on_top))
     def _():
@@ -360,24 +396,25 @@
     moments[...] = jnp.broadcast_to(out, moments.shape)
 
 
-def basis(fields, first, second, chip, far, far2, chip2, strip, devices):
+def basis(fields, halo, chip, far, chip2, strips, devices):
     rows, cols = fields[0].shape
     vmem = pl.BlockSpec(memory_space=pltpu.VMEM)
     out = jax.ShapeDtypeStruct((rows, cols), F32)
     return pl.pallas_call(
         _basis,
-        in_specs=[vmem] * 12,
+        in_specs=[vmem] * 10,
         out_specs=(vmem,) * 5,
         out_shape=(out,) * 4 + (jax.ShapeDtypeStruct((devices, LANES), F32),),
         scratch_shapes=[
             pltpu.VMEM((8, rows + 32, cols + LANES), F32),
             pltpu.VMEM((3, rows + 32, cols + LANES), F32),
             pltpu.VMEM((8, cols + LANES), F32),
-            pltpu.VMEM((4, 2 * STRIP, LANES), F32),
+            pltpu.VMEM((2, STRIP, cols), F32),
+            pltpu.VMEM((2, STRIP, LANES), F32),
         ],
         compiler_params=pltpu.CompilerParams(vmem_limit_bytes=GRANT),
         name="basis",
-    )(*fields, first, second, chip, far, far2, chip2, strip)
+    )(*fields, halo, chip, far, chip2, strips)
 
 
 def _combine(gathered, r, t1, t2, t3, t4, x_out, r_out):
@@ -483,12 +520,12 @@
                     pairs.append((i * lons + j, there[0] * lons + there[1] % lons))
         return lax.ppermute(x, LAT_LON, pairs)
 
-    def second_row(i, j):
-        if i == lats - 1:
-            return (i, lons - 1 - j)
-        if i == 0:
-            return None
-        return (i + 1 if i % 2 else i - 1, j)
+    def row_trade(i, j):
+        if (i + j) % 2:
+            return (i - 1, j) if i else None
+        if i < lats - 1:
+            return (i + 1, j)
+        return (i, lons - j) if j % 2 else None
 
     def off_chip(i, j):
         return (i, j + 1 if j % 2 else j - 1)
@@ -498,15 +535,15 @@
 
     top = (lats - 1,)
     kept = [pltpu.with_memory_space_constraint(x, pltpu.HBM) for x in (*fields, fold_partner.reshape(1, cols))]
-    to_first, to_second = pack_rows(kept[:5], kept[5])
-    first = swap(to_first, lambda i, j: (i ^ 1, j))
-    second = swap(to_second, second_row)
-    to_chip, to_far, strip = pack_cols(fields, first, second, to_second)
+    mine = pack_rows(kept[:5], kept[5])
+    sibling = swap(mine, on_chip)
+    traded = swap(pack_chip(mine, sibling), row_trade)
+    told = swap(traded, on_chip)
+    to_chip, to_far, halo, strips = pack_cols(fields, mine, sibling, traded, told)
+    far = swap(to_far, off_chip)
     chip = swap(to_chip, on_chip)
-    far = swap(to_far, off_chip)
-    far2 = swap(chip, off_chip, top)
     chip2 = swap(far, on_chip, top)
-    t1, t2, t3, t4, moments = basis(fields, first, second, chip, far, far2, chip2, strip, devices)
+    t1, t2, t3, t4, moments = basis(fields, halo, chip, far, chip2, strips, devices)
     gathered = lax.all_to_all(moments, LAT_LON, 0, 0)
     return combine(gathered, right_side, t1, t2, t3, t4)
 

time: 43.9 us -> 45.7 us (1.041)
  blocking collectives: 29.1 us -> 21.9 us
  starting transfers between devices: 7.84 us -> 13.8 us
  waiting for transfers between devices: 2.48 us -> 5.51 us
    all_to_all x1, blocking collectives: 29.1 us -> 21.9 us  [local(): gathered = lax.all_to_all(moments, LAT_LON, 0, 0)]
    ppermute x6, starting transfers between devices: 7.84 us -> 13.8 us  [swap(): return lax.ppermute(x, LAT_LON, pairs)]
    ppermute x6, waiting for transfers between devices: 2.48 us -> 5.51 us  [swap(): return lax.ppermute(x, LAT_LON, pairs)]
    pallas_call x2 -> x3, Pallas kernels: 1.46 us -> 1.47 us  [the longest x1 1.21 us: basis(): pl.pallas_call(_basis, in_specs=[vmem] * 10, out_specs=(vmem,) * 5, out_s...]
  transfers between devices with their start and end apart: 6 -> 6, of which waited for: 2 -> 4; matrix products, arithmetic and copies ran while one was open for 0% -> 0% of each run, Pallas kernels for 0% -> 0%
where the time goes in v4:
time: 45.7 us; the launch traced here: 45.5 us
  blocking collectives  21.9 us (48%)
  starting transfers between devices  13.8 us (30%)
  waiting for transfers between devices  5.51 us (12%)
  Pallas kernels  3.5 us (8%)
  between operations  0.73 us (2%)
    all_to_all x1, blocking collectives, local(): gathered = lax.all_to_all(moments, LAT_LON, 0, 0)  21.9 us
    ppermute x6, starting transfers between devices, swap(): return lax.ppermute(x, LAT_LON, pairs)  13.8 us
    ppermute x6, waiting for transfers between devices, swap(): return lax.ppermute(x, LAT_LON, pairs)  5.51 us
    pallas_call x1, Pallas kernels, basis(): pl.pallas_call(_basis, in_specs=[vmem] * 10, out_specs=(vmem,) * 5, out_s...  1.21 us
    pallas_call x1, Pallas kernels, combine(): pl.pallas_call(_combine, in_specs=[vmem] * 6, out_specs=(vmem,) * 2, out_...  1.08 us
    pallas_call x1, Pallas kernels, pack_rows(): pl.pallas_call(_pack_rows, in_specs=[pl.BlockSpec(memory_space=pltpu.HBM)...  0.95 us
  transfers between devices with their start and end apart: 6, of which 4 were waited for; matrix products, arithmetic and copies ran while one was open for 0% of the time, Pallas kernels for 0%

profile of v4, /device:TPU:1, one launch (start us, length us, event | category | flops | bytes accessed | tf_op | source)
XLA Modules:
  0.0 45.5 jit_solution(12083802275310802100)
XLA Ops:
  0.6 0.0 copy-start.1
  0.6 0.0 copy-start.2
  0.7 0.0 copy-start.3
  0.7 0.0 copy-start.4
  0.7 1.0 %pack_rows.1.mine = f32[48,256]{1,0:T(8,128)S(1)} custom-call(f32[128,256]{1,0:T(8,128)} %r.5, s32[128,256]{1,0:T(8,128)} %oc.3, f32[128,256]{1,0:T(8,128)} %dg.3, f32[128,256]{1,0:T(8,128)} %ea.3, f32[128,256]{1,0:T(8,128)} %no.3, s32[1,256]{1,0:T(1,128)} %bitcast.7), custom_call_target="tpu_custom_call" | custom-call | tf_op jit(solution)/shard_map/pack_rows/pallas_call | solution.py:56
  1.6 0.0 copy-start
  1.6 1.5 %collective-permute-start = (f32[48,256]{1,0:T(8,128)S(1)}, f32[48,256]{1,0:T(8,128)S(1)}, u32[]{:S(2)}, u32[]{:S(2)}) collective-permute-start(f32[48,256]{1,0:T(8,128)S(1)} %pack_rows.1.mine), channel_id=1, source_target_pairs={{0,1},{1,0},{2,3},{3,2},{4,5},{5,4},{6,7},{7,6},{8,9},{9,8},{10,11... | collective-permute-start | bytes 147464 | tf_op jit(solution)/shard_map/ppermute | solution.py:521
  3.1 0.9 %collective-permute-done.sibling = f32[48,256]{1,0:T(8,128)S(1)} collective-permute-done((f32[48,256]{1,0:T(8,128)S(1)}, f32[48,256]{1,0:T(8,128)S(1)}, u32[]{:S(2)}, u32[]{:S(2)}) %collective-permute-start) | collective-permute-done | bytes 49184 | tf_op jit(solution)/shard_map/ppermute | solution.py:521
  4.0 0.7 %collective-permute-start.1 = (f32[48,256]{1,0:T(8,128)S(1)}, f32[48,256]{1,0:T(8,128)S(1)}, u32[]{:S(2)}, u32[]{:S(2)}) collective-permute-start(f32[48,256]{1,0:T(8,128)S(1)} %pack_chip.1), channel_id=1, source_target_pairs={{0,16},{2,18},{4,20},{6,22},{8,24},{10,26},{12,28},{14,30},{16,0},... | collective-permute-start | bytes 147464 | tf_op jit(solution)/shard_map/ppermute | solution.py:521
  4.7 0.0 collective-permute-done.1.traded
  4.7 5.7 %collective-permute-start.2 = (f32[48,256]{1,0:T(8,128)S(1)}, f32[48,256]{1,0:T(8,128)S(1)}, u32[]{:S(2)}, u32[]{:S(2)}) collective-permute-start(f32[48,256]{1,0:T(8,128)S(1)} %collective-permute-done.1.traded), channel_id=1, source_target_pairs={{0,1},{1,0},{2,3},{3,2},{4,5},{5,4},{6,7},{7,6},{8,9},{9,8},{10,11... | collective-permute-start | bytes 147464 | tf_op jit(solution)/shard_map/ppermute | solution.py:521
  10.3 0.9 %collective-permute-done.2.told = f32[48,256]{1,0:T(8,128)S(1)} collective-permute-done((f32[48,256]{1,0:T(8,128)S(1)}, f32[48,256]{1,0:T(8,128)S(1)}, u32[]{:S(2)}, u32[]{:S(2)}) %collective-permute-start.2) | collective-permute-done | bytes 49184 | tf_op jit(solution)/shard_map/ppermute | solution.py:521
  11.2 0.0 copy-done.1
  11.2 0.0 copy-done.3
  11.2 0.2 pack_cols.1
  11.5 2.1 %collective-permute-start.4 = (f32[288,128]{1,0:T(8,128)S(1)}, f32[288,128]{1,0:T(8,128)S(1)}, u32[]{:S(2)}, u32[]{:S(2)}) collective-permute-start(f32[288,128]{1,0:T(8,128)S(1)} %get-tuple-element.13), channel_id=1, source_target_pairs={{0,15},{1,2},{2,1},{3,4},{4,3},{5,6},{6,5},{7,8},{8,7},{9,10},{10,... | collective-permute-start | bytes 442376 | tf_op jit(solution)/shard_map/ppermute | solution.py:521
  13.6 2.8 %collective-permute-done.4.far = f32[288,128]{1,0:T(8,128)S(1)} collective-permute-done((f32[288,128]{1,0:T(8,128)S(1)}, f32[288,128]{1,0:T(8,128)S(1)}, u32[]{:S(2)}, u32[]{:S(2)}) %collective-permute-start.4) | collective-permute-done | bytes 147488 | tf_op jit(solution)/shard_map/ppermute | solution.py:521
  16.4 0.7 %collective-permute-start.5 = (f32[288,128]{1,0:T(8,128)S(1)}, f32[288,128]{1,0:T(8,128)S(1)}, u32[]{:S(2)}, u32[]{:S(2)}) collective-permute-start(f32[288,128]{1,0:T(8,128)S(1)} %collective-permute-done.4.far), channel_id=1, source_target_pairs={{112,113},{113,112},{114,115},{115,114},{116,117},{117,116},{118,1... | collective-permute-start | bytes 442376 | tf_op jit(solution)/shard_map/ppermute | solution.py:521
  17.1 3.3 %collective-permute-start.3 = (f32[144,128]{1,0:T(8,128)S(1)}, f32[144,128]{1,0:T(8,128)S(1)}, u32[]{:S(2)}, u32[]{:S(2)}) collective-permute-start(f32[144,128]{1,0:T(8,128)S(1)} %get-tuple-element.12), channel_id=1, source_target_pairs={{0,1},{1,0},{2,3},{3,2},{4,5},{5,4},{6,7},{7,6},{8,9},{9,8},{10,11... | collective-permute-start | bytes 221192 | tf_op jit(solution)/shard_map/ppermute | solution.py:521
  20.3 0.9 %collective-permute-done.3.chip = f32[144,128]{1,0:T(8,128)S(1)} collective-permute-done((f32[144,128]{1,0:T(8,128)S(1)}, f32[144,128]{1,0:T(8,128)S(1)}, u32[]{:S(2)}, u32[]{:S(2)}) %collective-permute-start.3) | collective-permute-done | bytes 73760 | tf_op jit(solution)/shard_map/ppermute | solution.py:521
  21.3 0.0 collective-permute-done.5.chip2
  21.3 1.2 %basis.1 = (f32[128,256]{1,0:T(8,128)S(1)}, f32[128,256]{1,0:T(8,128)S(1)}, f32[128,256]{1,0:T(8,128)S(1)}, f32[128,256]{1,0:T(8,128)S(1)}, f32[128,128]{1,0:T(8,128)S(1)}) custom-call(f32[128,256]{1,0:T(8,128)S(1)} %copy-done, s32[128,256]{1,0:T(8,128)S(1)} %copy-done.1, f32[128,256]{1,0:T(8,128)S(1)} %copy-done.2, f32[128,256]{1,0:T(8,128)S(1)} %copy-done.3, ...), custom_call_target="tpu_custom_call" | custom-call | tf_op jit(solution)/shard_map/basis/pallas_call | solution.py:403
  22.5 21.9 %all_to_all.11 = f32[128,1,128]{2,1,0:T(1,128)S(1)} all-to-all(f32[128,1,128]{2,1,0:T(1,128)S(1)} %bitcast.6), channel_id=1, replica_groups=mesh['lat_0'=2,'lat_1'=4,'lon_0'=2,'lon_1'=4,'lon_2'=2] {'lat_0','lat_1'..., dimensions={0} | all-to-all | bytes 131072 | tf_op jit(solution)/shard_map/all_to_all | solution.py:547
  44.4 1.1 %combine.1 = (f32[128,256]{1,0:T(8,128)}, f32[128,256]{1,0:T(8,128)}) custom-call(f32[128,128]{1,0:T(8,128)S(1)} %bitcast.5, f32[128,256]{1,0:T(8,128)S(1)} %copy-done, f32[128,256]{1,0:T(8,128)S(1)} %get-tuple-element.16.t1, f32[128,256]{1,0:T(8,128)S(1)} %get-tuple-element.17.t2, f32[128,256]{1,0:T(8,128)S(1)} %get-tuple-element.18.t3, ...), custom_call_target="tpu_custom_call" | custom-call | tf_op jit(solution)/shard_map/combine/pallas_call | solution.py:498
  (4 shorter events, 0.0 us)
Async XLA Ops:
  0.6 10.6 %copy-start.1 = (s32[128,256]{1,0:T(8,128)S(1)}, s32[128,256]{1,0:T(8,128)}, u32[]{:S(2)}) copy-start(s32[128,256]{1,0:T(8,128)} %oc.3) | copy-start | bytes 393220
  0.6 10.6 %copy-start.2 = (f32[128,256]{1,0:T(8,128)S(1)}, f32[128,256]{1,0:T(8,128)}, u32[]{:S(2)}) copy-start(f32[128,256]{1,0:T(8,128)} %dg.3) | copy-start | bytes 393220
  0.7 10.6 %copy-start.3 = (f32[128,256]{1,0:T(8,128)S(1)}, f32[128,256]{1,0:T(8,128)}, u32[]{:S(2)}) copy-start(f32[128,256]{1,0:T(8,128)} %ea.3) | copy-start | bytes 393220
  0.7 10.6 %copy-start.4 = (f32[128,256]{1,0:T(8,128)S(1)}, f32[128,256]{1,0:T(8,128)}, u32[]{:S(2)}) copy-start(f32[128,256]{1,0:T(8,128)} %no.3) | copy-start | bytes 393220
  1.6 9.6 %copy-start = (f32[128,256]{1,0:T(8,128)S(1)}, f32[128,256]{1,0:T(8,128)}, u32[]{:S(2)}) copy-start(f32[128,256]{1,0:T(8,128)} %r.5) | copy-start | bytes 393220
  1.6 2.3 %collective-permute-start = (f32[48,256]{1,0:T(8,128)S(1)}, f32[48,256]{1,0:T(8,128)S(1)}, u32[]{:S(2)}, u32[]{:S(2)}) collective-permute-start(f32[48,256]{1,0:T(8,128)S(1)} %pack_rows.1.mine), channel_id=1, source_target_pairs={{0,1},{1,0},{2,3},{3,2},{4,5},{5,4},{6,7},{7,6},{8,9},{9,8},{10,11... | collective-permute-start | bytes 147464 | tf_op jit(solution)/shard_map/ppermute | solution.py:521
  4.0 0.7 %collective-permute-start.1 = (f32[48,256]{1,0:T(8,128)S(1)}, f32[48,256]{1,0:T(8,128)S(1)}, u32[]{:S(2)}, u32[]{:S(2)}) collective-permute-start(f32[48,256]{1,0:T(8,128)S(1)} %pack_chip.1), channel_id=1, source_target_pairs={{0,16},{2,18},{4,20},{6,22},{8,24},{10,26},{12,28},{14,30},{16,0},... | collective-permute-start | bytes 147464 | tf_op jit(solution)/shard_map/ppermute | solution.py:521
  4.7 6.5 %collective-permute-start.2 = (f32[48,256]{1,0:T(8,128)S(1)}, f32[48,256]{1,0:T(8,128)S(1)}, u32[]{:S(2)}, u32[]{:S(2)}) collective-permute-start(f32[48,256]{1,0:T(8,128)S(1)} %collective-permute-done.1.traded), channel_id=1, source_target_pairs={{0,1},{1,0},{2,3},{3,2},{4,5},{5,4},{6,7},{7,6},{8,9},{9,8},{10,11... | collective-permute-start | bytes 147464 | tf_op jit(solution)/shard_map/ppermute | solution.py:521
  11.5 4.9 %collective-permute-start.4 = (f32[288,128]{1,0:T(8,128)S(1)}, f32[288,128]{1,0:T(8,128)S(1)}, u32[]{:S(2)}, u32[]{:S(2)}) collective-permute-start(f32[288,128]{1,0:T(8,128)S(1)} %get-tuple-element.13), channel_id=1, source_target_pairs={{0,15},{1,2},{2,1},{3,4},{4,3},{5,6},{6,5},{7,8},{8,7},{9,10},{10,... | collective-permute-start | bytes 442376 | tf_op jit(solution)/shard_map/ppermute | solution.py:521
  16.4 4.9 %collective-permute-start.5 = (f32[288,128]{1,0:T(8,128)S(1)}, f32[288,128]{1,0:T(8,128)S(1)}, u32[]{:S(2)}, u32[]{:S(2)}) collective-permute-start(f32[288,128]{1,0:T(8,128)S(1)} %collective-permute-done.4.far), channel_id=1, source_target_pairs={{112,113},{113,112},{114,115},{115,114},{116,117},{117,116},{118,1... | collective-permute-start | bytes 442376 | tf_op jit(solution)/shard_map/ppermute | solution.py:521
  17.1 4.2 %collective-permute-start.3 = (f32[144,128]{1,0:T(8,128)S(1)}, f32[144,128]{1,0:T(8,128)S(1)}, u32[]{:S(2)}, u32[]{:S(2)}) collective-permute-start(f32[144,128]{1,0:T(8,128)S(1)} %get-tuple-element.12), channel_id=1, source_target_pairs={{0,1},{1,0},{2,3},{3,2},{4,5},{5,4},{6,7},{7,6},{8,9},{9,8},{10,11... | collective-permute-start | bytes 221192 | tf_op jit(solution)/shard_map/ppermute | solution.py:521

commit v5 on v3

--- a/solution.py
+++ b/solution.py
@@ -12,8 +12,9 @@
 LAT_LON = ("lat_0", "lat_1", "lon_0", "lon_1", "lon_2")
 LAT = ("lat_0", "lat_1")
 LON = ("lon_0", "lon_1", "lon_2")
-MID = 4.6
-HALF = 4.4
+MID = 4.3
+HALF = 4.1
+LIMIT = 12.0
 F32 = jnp.float32
 W = 4
 LANES = 128
@@ -346,12 +347,9 @@
                 outs[k][a - pad : a - pad + 8, :] = mine
                 x = mine * v[:, :cols]
                 cross = x if cross is None else cross + x
-                if k < 3:
-                    s = mine * mine
-                    square = s if square is None else square + s
-        sums.append(cross)
-        if k < 3:
-            sums.append(square)
+                s = mine * mine
+                square = s if square is None else square + s
+        sums += [cross, square]
     out = jnp.zeros((1, LANES), F32)
     for k, x in enumerate(sums):
         folded = x[:, :LANES] + x[:, LANES:]
@@ -380,14 +378,15 @@
     )(*fields, first, second, chip, far, far2, chip2, strip)
 
 
-def _combine(gathered, r, t1, t2, t3, t4, x_out, r_out):
+def _combine(gathered, r, t1, t2, t3, t4, x_out, r_out, weak):
     sums = jnp.sum(gathered[...], axis=0, keepdims=True)
-    m = [sums[:, k : k + 1] for k in range(8)]
+    m = [sums[:, k : k + 1] for k in range(9)]
     nu = [m[0], m[1]]
     for k in range(1, 4):
         nu += [2.0 * m[2 * k] - m[0], 2.0 * m[2 * k + 1] - m[1]]
+    nu.append(2.0 * m[8] - m[0])
     gram = {}
-    for i in range(4):
+    for i in range(5):
         for j in range(i, 5):
             if i == 0:
                 gram[i, j] = nu[j]
@@ -441,6 +440,10 @@
             norm_next = dot(residual, residual)
             direction = add(residual, norm_next / norm_now, direction)
             norm_now = norm_next
+    size = dot(residual, residual)
+    largest = functools.reduce(jnp.maximum, (residual[k] * residual[k] * m[2 * k] for k in range(5)))
+    good = largest <= (LIMIT * LIMIT) * size
+    weak[0, 0] = 1 - jnp.max(good.astype(jnp.int32))
     basis_refs = (r, t1, t2, t3, t4)
     for start in range(0, r.shape[0], 8):
         span = pl.ds(start, 8)
@@ -461,11 +464,67 @@
     return pl.pallas_call(
         _combine,
         in_specs=[vmem] * 6,
-        out_specs=(vmem,) * 2,
-        out_shape=(out, out),
+        out_specs=(vmem, vmem, pl.BlockSpec(memory_space=pltpu.SMEM)),
+        out_shape=(out, out, jax.ShapeDtypeStruct((1, 1), jnp.int32)),
         compiler_params=pltpu.CompilerParams(vmem_limit_bytes=GRANT),
         name="combine",
     )(gathered, r, t1, t2, t3, t4)
+
+
+def shifted(x, axes, dim, up):
+    count, length = (lax.axis_size(axes), x.shape[dim])
+    ring = [(i, (i + 1) % count) if up else ((i + 1) % count, i) for i in range(count)]
+    edge = lax.slice_in_dim(x, length - 1, length, axis=dim) if up else lax.slice_in_dim(x, 0, 1, axis=dim)
+    edge = lax.ppermute(edge, axes, ring)
+    if up:
+        return _cat([edge, lax.slice_in_dim(x, 0, length - 1, axis=dim)], dim)
+    return _cat([lax.slice_in_dim(x, 1, length, axis=dim), edge], dim)
+
+
+def classic(right_side, diagonal, east_coef, north_coef, land_sea, fold_partner):
+    row_count, col_count = right_side.shape
+    ocean = land_sea.astype(F32)
+    on_top = lax.axis_index(LAT) == lax.axis_size(LAT) - 1
+    top_row = on_top & (_iota((row_count, 1), 0) == row_count - 1)
+    north_inner = jnp.where(top_row, 0.0, north_coef)
+    west_coef = shifted(east_coef, LON, 1, True)
+    south_coef = shifted(north_inner, LAT, 0, True)
+    lons = lax.axis_size(LON)
+    columns = fold_partner.astype(jnp.int32) - (lons - 1 - lax.axis_index(LON)) * col_count
+
+    def mirrored(row):
+        row = lax.ppermute(row, LON, [(j, lons - 1 - j) for j in range(lons)])
+        return jnp.take(row, columns, axis=0)
+
+    top_coef = north_coef[row_count - 1]
+    fold_coef = 0.5 * (top_coef + mirrored(top_coef))
+
+    def operate(surface):
+        masked = ocean * surface
+        spread = east_coef * (masked - shifted(masked, LON, 1, False))
+        spread = spread + west_coef * (masked - shifted(masked, LON, 1, True))
+        spread = spread + north_inner * (masked - shifted(masked, LAT, 0, False))
+        spread = spread + south_coef * (masked - shifted(masked, LAT, 0, True))
+        last = masked[row_count - 1]
+        fold = fold_coef * (last - mirrored(last))
+        spread = spread + jnp.where(top_row, fold[None, :], 0.0)
+        return diagonal * surface + ocean * spread
+
+    def total(x):
+        return functools.reduce(lax.psum, LAT_LON, jnp.sum(x))
+
+    def step(_, state):
+        solution_field, residual, direction, norm_now = state
+        image = operate(direction)
+        alpha = norm_now / total(direction * image)
+        solution_field = solution_field + alpha * direction
+        residual = residual - alpha * image
+        norm_next = total(residual * residual)
+        direction = residual + (norm_next / norm_now) * direction
+        return (solution_field, residual, direction, norm_next)
+
+    state = (jnp.zeros_like(right_side), right_side, right_side, total(right_side * right_side))
+    return lax.fori_loop(0, ITERS, step, state)[:2]
 
 
 def local(right_side, diagonal, east_coef, north_coef, land_sea, fold_partner):
@@ -508,7 +567,13 @@
     chip2 = swap(far, on_chip, top)
     t1, t2, t3, t4, moments = basis(fields, first, second, chip, far, far2, chip2, strip, devices)
     gathered = lax.all_to_all(moments, LAT_LON, 0, 0)
-    return combine(gathered, right_side, t1, t2, t3, t4)
+    solution_field, residual, weak = combine(gathered, right_side, t1, t2, t3, t4)
+
+    def again(state):
+        return (jnp.int32(0), *classic(right_side, diagonal, east_coef, north_coef, land_sea, to_second[20]))
+
+    state = (weak[0, 0], solution_field, residual)
+    return lax.while_loop(lambda state: state[0] > 0, again, state)[1:]
 
 
 def solution(mesh):

time: 43.9 us -> 44.6 us (1.016)
  loops' own time: 0 us -> 0.64 us
    another operation x0 -> x1, loops' own time: none -> 0.64 us  [local(): return lax.while_loop(lambda state: state[0] > 0, again, state)[1:]]
where the time goes in v5:
time: 44.6 us; the launch traced here: 44.4 us
  blocking collectives  29.1 us (65%)
  starting transfers between devices  7.84 us (18%)
  Pallas kernels  3.54 us (8%)
  waiting for transfers between devices  2.48 us (6%)
  between operations  0.77 us (2%)
  loops' own time  0.64 us (1%)
    all_to_all x1, blocking collectives, local(): gathered = lax.all_to_all(moments, LAT_LON, 0, 0)  29.1 us
    ppermute x6, starting transfers between devices, swap(): return lax.ppermute(x, LAT_LON, pairs)  7.84 us
    ppermute x6, waiting for transfers between devices, swap(): return lax.ppermute(x, LAT_LON, pairs)  2.48 us
    pallas_call x1, Pallas kernels, basis(): pl.pallas_call(_basis, in_specs=[vmem] * 12, out_specs=(vmem,) * 5, out_s...  1.22 us
    pallas_call x1, Pallas kernels, combine(): pl.pallas_call(_combine, in_specs=[vmem] * 6, out_specs=(vmem, vmem, pl.B...  1.09 us
    pallas_call x1, Pallas kernels, pack_rows(): pl.pallas_call(_pack_rows, in_specs=[pl.BlockSpec(memory_space=pltpu.HBM)...  0.99 us
  transfers between devices with their start and end apart: 6, of which 2 were waited for; matrix products, arithmetic and copies ran while one was open for 0% of the time, Pallas kernels for 0%

profile of v5, /device:TPU:1, one launch (start us, length us, event | category | flops | bytes accessed | tf_op | source)
XLA Modules:
  0.0 44.4 jit_solution(2845398871818462145)
XLA Ops:
  0.6 0.0 copy-start.1
  0.6 0.0 copy-start.2
  0.7 0.0 copy-start.4
  0.7 0.0 copy-start.5
  0.7 0.0 copy-start.6
  0.7 1.0 %pack_rows.1 = (f32[24,256]{1,0:T(8,128)S(1)}, f32[24,256]{1,0:T(8,128)S(1)}) custom-call(f32[128,256]{1,0:T(8,128)} %r.5, s32[128,256]{1,0:T(8,128)} %oc.3, f32[128,256]{1,0:T(8,128)} %dg.3, f32[128,256]{1,0:T(8,128)} %ea.3, f32[128,256]{1,0:T(8,128)} %no.3, s32[1,256]{1,0:T(1,128)} %bitcast.28), custom_call_target="tpu_custom_call" | custom-call | tf_op jit(solution)/shard_map/pack_rows/pallas_call | solution.py:62
  1.7 2.2 %collective-permute-start.8 = (f32[24,256]{1,0:T(8,128)S(1)}, f32[24,256]{1,0:T(8,128)S(1)}, u32[]{:S(2)}, u32[]{:S(2)}) collective-permute-start(f32[24,256]{1,0:T(8,128)S(1)} %get-tuple-element.167), channel_id=1, source_target_pairs={{0,16},{1,17},{2,18},{3,19},{4,20},{5,21},{6,22},{7,23},{8,24},{9,... | collective-permute-start | bytes 73736 | tf_op jit(solution)/shard_map/ppermute | solution.py:543
  3.9 0.7 %collective-permute-start.9 = (f32[24,256]{1,0:T(8,128)S(1)}, f32[24,256]{1,0:T(8,128)S(1)}, u32[]{:S(2)}, u32[]{:S(2)}) collective-permute-start(f32[24,256]{1,0:T(8,128)S(1)} %get-tuple-element.467.own_top), channel_id=1, source_target_pairs={{16,32},{17,33},{18,34},{19,35},{20,36},{21,37},{22,38},{23,39},{2... | collective-permute-start | bytes 73736 | tf_op jit(solution)/shard_map/ppermute | solution.py:543
  4.5 0.6 %collective-permute-done.8.first = f32[24,256]{1,0:T(8,128)S(1)} collective-permute-done((f32[24,256]{1,0:T(8,128)S(1)}, f32[24,256]{1,0:T(8,128)S(1)}, u32[]{:S(2)}, u32[]{:S(2)}) %collective-permute-start.8) | collective-permute-done | bytes 24608 | tf_op jit(solution)/shard_map/ppermute | solution.py:543
  5.1 0.0 collective-permute-done.9.second
  5.1 0.0 copy-done.1
  5.1 0.2 pack_cols.1
  5.4 2.0 %collective-permute-start.10 = (f32[240,128]{1,0:T(8,128)S(1)}, f32[240,128]{1,0:T(8,128)S(1)}, u32[]{:S(2)}, u32[]{:S(2)}) collective-permute-start(f32[240,128]{1,0:T(8,128)S(1)} %get-tuple-element.169), channel_id=1, source_target_pairs={{0,1},{1,0},{2,3},{3,2},{4,5},{5,4},{6,7},{7,6},{8,9},{9,8},{10,11... | collective-permute-start | bytes 368648 | tf_op jit(solution)/shard_map/ppermute | solution.py:543
  7.3 1.7 %collective-permute-start.11 = (f32[240,128]{1,0:T(8,128)S(1)}, f32[240,128]{1,0:T(8,128)S(1)}, u32[]{:S(2)}, u32[]{:S(2)}) collective-permute-start(f32[240,128]{1,0:T(8,128)S(1)} %get-tuple-element.170), channel_id=1, source_target_pairs={{0,15},{1,2},{2,1},{3,4},{4,3},{5,6},{6,5},{7,8},{8,7},{9,10},{10,... | collective-permute-start | bytes 368648 | tf_op jit(solution)/shard_map/ppermute | solution.py:543
  9.1 0.0 collective-permute-done.10.chip
  9.1 0.7 %collective-permute-start.12 = (f32[240,128]{1,0:T(8,128)S(1)}, f32[240,128]{1,0:T(8,128)S(1)}, u32[]{:S(2)}, u32[]{:S(2)}) collective-permute-start(f32[240,128]{1,0:T(8,128)S(1)} %collective-permute-done.10.chip), channel_id=1, source_target_pairs={{112,127},{113,114},{114,113},{115,116},{116,115},{117,118},{118,1... | collective-permute-start | bytes 368648 | tf_op jit(solution)/shard_map/ppermute | solution.py:543
  9.7 1.9 %collective-permute-done.11.far = f32[240,128]{1,0:T(8,128)S(1)} collective-permute-done((f32[240,128]{1,0:T(8,128)S(1)}, f32[240,128]{1,0:T(8,128)S(1)}, u32[]{:S(2)}, u32[]{:S(2)}) %collective-permute-start.11) | collective-permute-done | bytes 122912 | tf_op jit(solution)/shard_map/ppermute | solution.py:543
  11.6 0.7 %collective-permute-start.13 = (f32[240,128]{1,0:T(8,128)S(1)}, f32[240,128]{1,0:T(8,128)S(1)}, u32[]{:S(2)}, u32[]{:S(2)}) collective-permute-start(f32[240,128]{1,0:T(8,128)S(1)} %collective-permute-done.11.far), channel_id=1, source_target_pairs={{112,113},{113,112},{114,115},{115,114},{116,117},{117,116},{118,1... | collective-permute-start | bytes 368648 | tf_op jit(solution)/shard_map/ppermute | solution.py:543
  12.3 0.0 collective-permute-done.12.far2
  12.3 0.0 collective-permute-done.13.chip2
  12.3 1.2 %basis.1 = (f32[128,256]{1,0:T(8,128)S(1)}, f32[128,256]{1,0:T(8,128)S(1)}, f32[128,256]{1,0:T(8,128)S(1)}, f32[128,256]{1,0:T(8,128)S(1)}, f32[128,128]{1,0:T(8,128)S(1)}) custom-call(f32[128,256]{1,0:T(8,128)S(1)} %copy-done.4, s32[128,256]{1,0:T(8,128)S(1)} %copy-done.6, f32[128,256]{1,0:T(8,128)S(1)} %copy-done.2, f32[128,256]{1,0:T(8,128)S(1)} %copy-done.1, ...), custom_call_target="tpu_custom_call" | custom-call | tf_op jit(solution)/shard_map/basis/pallas_call | solution.py:365
  13.5 29.1 %all_to_all.11 = f32[128,1,128]{2,1,0:T(1,128)S(1)} all-to-all(f32[128,1,128]{2,1,0:T(1,128)S(1)} %bitcast.18), channel_id=1, replica_groups=mesh['lat_0'=2,'lat_1'=4,'lon_0'=2,'lon_1'=4,'lon_2'=2] {'lat_0','lat_1'..., dimensions={0} | all-to-all | bytes 131072 | tf_op jit(solution)/shard_map/all_to_all | solution.py:569
  42.7 1.1 %combine.1 = (f32[128,256]{1,0:T(8,128)}, f32[128,256]{1,0:T(8,128)}, s32[1,1]{1,0:T(1,128)}) custom-call(f32[128,128]{1,0:T(8,128)S(1)} %bitcast.17, f32[128,256]{1,0:T(8,128)S(1)} %copy-done.4, f32[128,256]{1,0:T(8,128)S(1)} %get-tuple-element.173.t1, f32[128,256]{1,0:T(8,128)S(1)} %get-tuple-element.174.t2, f32[128,256]{1,0:T(8,128)S(1)} %get-tuple-element.175.t3, ...), custom_call_target="tpu_custom_call" | custom-call | tf_op jit(solution)/shard_map/combine/pallas_call | solution.py:464
  43.8 0.6 %while.28 = (s32[]{:T(128)}, f32[128,256]{1,0:T(8,128)}, f32[128,256]{1,0:T(8,128)}, f32[128,256]{1,0:T(8,128)S(1)}, s32[128,256]{1,0:T(8,128)S(1)}, /*index=5*/...) while((s32[]{:T(128)}, f32[128,256]{1,0:T(8,128)}, ...), condition=%region_21.23_spmd, body=%region_0.22_spmd | while | flops 1254441 | bytes 7013051 | solution.py:576
  (4 shorter events, 0.0 us)
Async XLA Ops:
  0.6 4.5 %copy-start.1 = (f32[128,256]{1,0:T(8,128)S(1)}, f32[128,256]{1,0:T(8,128)}, u32[]{:S(2)}) copy-start(f32[128,256]{1,0:T(8,128)} %ea.3) | copy-start | bytes 393220
  0.6 4.5 %copy-start.2 = (f32[128,256]{1,0:T(8,128)S(1)}, f32[128,256]{1,0:T(8,128)}, u32[]{:S(2)}) copy-start(f32[128,256]{1,0:T(8,128)} %dg.3) | copy-start | bytes 393220
  0.7 4.4 %copy-start.4 = (f32[128,256]{1,0:T(8,128)S(1)}, f32[128,256]{1,0:T(8,128)}, u32[]{:S(2)}) copy-start(f32[128,256]{1,0:T(8,128)} %r.5) | copy-start | bytes 393220
  0.7 4.4 %copy-start.5 = (f32[128,256]{1,0:T(8,128)S(1)}, f32[128,256]{1,0:T(8,128)}, u32[]{:S(2)}) copy-start(f32[128,256]{1,0:T(8,128)} %no.3) | copy-start | bytes 393220
  0.7 4.4 %copy-start.6 = (s32[128,256]{1,0:T(8,128)S(1)}, s32[128,256]{1,0:T(8,128)}, u32[]{:S(2)}) copy-start(s32[128,256]{1,0:T(8,128)} %oc.3) | copy-start | bytes 393220
  1.7 3.4 %collective-permute-start.8 = (f32[24,256]{1,0:T(8,128)S(1)}, f32[24,256]{1,0:T(8,128)S(1)}, u32[]{:S(2)}, u32[]{:S(2)}) collective-permute-start(f32[24,256]{1,0:T(8,128)S(1)} %get-tuple-element.167), channel_id=1, source_target_pairs={{0,16},{1,17},{2,18},{3,19},{4,20},{5,21},{6,22},{7,23},{8,24},{9,... | collective-permute-start | bytes 73736 | tf_op jit(solution)/shard_map/ppermute | solution.py:543
  3.9 1.2 %collective-permute-start.9 = (f32[24,256]{1,0:T(8,128)S(1)}, f32[24,256]{1,0:T(8,128)S(1)}, u32[]{:S(2)}, u32[]{:S(2)}) collective-permute-start(f32[24,256]{1,0:T(8,128)S(1)} %get-tuple-element.467.own_top), channel_id=1, source_target_pairs={{16,32},{17,33},{18,34},{19,35},{20,36},{21,37},{22,38},{23,39},{2... | collective-permute-start | bytes 73736 | tf_op jit(solution)/shard_map/ppermute | solution.py:543
  5.4 3.7 %collective-permute-start.10 = (f32[240,128]{1,0:T(8,128)S(1)}, f32[240,128]{1,0:T(8,128)S(1)}, u32[]{:S(2)}, u32[]{:S(2)}) collective-permute-start(f32[240,128]{1,0:T(8,128)S(1)} %get-tuple-element.169), channel_id=1, source_target_pairs={{0,1},{1,0},{2,3},{3,2},{4,5},{5,4},{6,7},{7,6},{8,9},{9,8},{10,11... | collective-permute-start | bytes 368648 | tf_op jit(solution)/shard_map/ppermute | solution.py:543
  7.3 4.3 %collective-permute-start.11 = (f32[240,128]{1,0:T(8,128)S(1)}, f32[240,128]{1,0:T(8,128)S(1)}, u32[]{:S(2)}, u32[]{:S(2)}) collective-permute-start(f32[240,128]{1,0:T(8,128)S(1)} %get-tuple-element.170), channel_id=1, source_target_pairs={{0,15},{1,2},{2,1},{3,4},{4,3},{5,6},{6,5},{7,8},{8,7},{9,10},{10,... | collective-permute-start | bytes 368648 | tf_op jit(solution)/shard_map/ppermute | solution.py:543
  9.1 3.2 %collective-permute-start.12 = (f32[240,128]{1,0:T(8,128)S(1)}, f32[240,128]{1,0:T(8,128)S(1)}, u32[]{:S(2)}, u32[]{:S(2)}) collective-permute-start(f32[240,128]{1,0:T(8,128)S(1)} %collective-permute-done.10.chip), channel_id=1, source_target_pairs={{112,127},{113,114},{114,113},{115,116},{116,115},{117,118},{118,1... | collective-permute-start | bytes 368648 | tf_op jit(solution)/shard_map/ppermute | solution.py:543
  11.6 0.7 %collective-permute-start.13 = (f32[240,128]{1,0:T(8,128)S(1)}, f32[240,128]{1,0:T(8,128)S(1)}, u32[]{:S(2)}, u32[]{:S(2)}) collective-permute-start(f32[240,128]{1,0:T(8,128)S(1)} %collective-permute-done.11.far), channel_id=1, source_target_pairs={{112,113},{113,112},{114,115},{115,114},{116,117},{117,116},{118,1... | collective-permute-start | bytes 368648 | tf_op jit(solution)/shard_map/ppermute | solution.py:543
